TPU v7x, 32 devices: a whole 2x2x4 slice. The times are simulated.
32 devices in a mesh: seg: 8 (over z, core), head: 4 (over y, x).
Axes of the slice: x: 2, y: 2, z: 4, core: 2. Of those that a mesh axis runs over, the one named last changes fastest.
Arguments:
- inputs: bfloat16 [8, 256, 16384], P('seg', None, 'head'), may hold values from -6 to 6
- deltas: float32 [8, 256, 256], P('seg', 'head'), may hold values from 0.01 to 0.1
- rates: float32 [256], P('head'), may hold values from 0.001 to 2
- skips: float32 [256], P('head'), may hold values from 0.5 to 1.5
- writer: bfloat16 [8, 256, 1024], P('seg'), may hold values from -1.796875 to 1.796875
- reader: bfloat16 [8, 256, 1024], P('seg'), may hold values from -1.796875 to 1.796875
- grad_out: bfloat16 [8, 256, 16384], P('seg', None, 'head'), may hold values from -6 to 6
- parents: int32 [8], replicated, may hold values from -1 to 7, as said below
- levels: int32 [8], replicated, may hold values from 0 to 2, as said below
Outputs:
- outputs: bfloat16 [8, 256, 16384], P('seg', None, 'head')
- grad_inputs: bfloat16 [8, 256, 16384], P('seg', None, 'head')
- grad_deltas: float32 [8, 256, 256], P('seg', 'head')
- grad_writer: bfloat16 [8, 256, 1024], P('seg', 'head')
- grad_reader: bfloat16 [8, 256, 1024], P('seg', 'head')
Inputs may be any that keep to these rules, and one draw needn't show every extreme that they name: `parents`: roots have parent -1 and level 0; every other segment's parent has a level one less than its own. A segment has at most four children, and some segment has level 2. levels[s] is the number of ancestors of segment s.
All inputs are finite; a program needn't handle non-finite values.
Results may differ from a plain program's by a relative error of at most 0.0046.
Values may be sent and summed in bfloat16 or wider, within the bound.
No kernel may reach another device: no remote copies, remote signals or barrier semaphores. Data moves between devices by JAX's collectives and lax.ppermute only.
A program may use at most 128 MiB of HBM per device.

v0:
```python
import functools

import jax
import jax.numpy as jnp
from jax import lax
from jax.experimental import pallas as pl
from jax.experimental.pallas import tpu as pltpu
from jax.sharding import PartitionSpec as P


H = 256
P_SIZE = 64
N = 128
G = 8
DEPTH = 3
TILE = 256
SLOTS = 64
LANES = 128
EXTRA = 16
PIECES = 2

F32 = jnp.float32
BF16 = jnp.bfloat16


def dot(a, b, dims=((1,), (0,))):
    return lax.dot_general(a, b, (dims, ((), ())), preferred_element_type=F32)


NT = ((1,), (1,))


def split(value, parts):
    pieces = []
    for _ in range(parts):
        piece = value.astype(BF16)
        pieces.append(piece)
        value = value - piece.astype(F32)
    return pieces


def iota(shape, axis):
    return lax.broadcasted_iota(jnp.int32, shape, axis)


def onehot(cond):
    return jnp.where(cond, 1.0, 0.0).astype(BF16)


def spread(step):
    shape = (2 * SLOTS, TILE)
    head = step * (TILE // P_SIZE) + iota(shape, 1) // P_SIZE
    return onehot((iota(shape, 0) % SLOTS) == head)


def local_kernel(
    per_group,
    _,
    x_ref,
    dy_ref,
    delta_ref,
    rate_ref,
    b_ref,
    c_ref,
    u_ref,
    v_ref,
    xs_ref,
    ys_ref,
    table_ref,
    low_ref,
    up_ref,
    gb_ref,
    gc_ref,
    acc_ref,
):
    step = pl.program_id(0)
    length = x_ref.shape[0]
    square = (length, length)

    @pl.when(step == 0)
    def _():
        tri = onehot(iota(square, 0) >= iota(square, 1))
        eye = onehot(iota(square, 0) == iota(square, 1))
        pieces = split(delta_ref[...], 3)
        sums = sum(dot(tri, piece, NT) for piece in pieces)
        delta = sum(dot(eye, piece, NT) for piece in pieces)
        log = rate_ref[...] * sums
        grow = split(jnp.exp(log) * delta, 2)
        fall = split(jnp.exp(-log), 2)
        table_ref[0] = jnp.concatenate(fall, axis=1)
        table_ref[1] = jnp.concatenate(grow, axis=1)

    lanes = spread(step)
    fall = dot(table_ref[0], lanes)
    grow = dot(table_ref[1], lanes)
    xs, xs_low = split(x_ref[...].astype(F32) * grow, 2)
    ys, ys_low = split(dy_ref[...].astype(F32) * fall, 2)
    xs_ref[...] = xs
    ys_ref[...] = ys
    b, c = b_ref[...], c_ref[...]
    u = dot(b, xs, ((0,), (0,))) + dot(b, xs_low, ((0,), (0,)))
    v = dot(c, ys, ((0,), (0,))) + dot(c, ys_low, ((0,), (0,)))
    u_ref[...] = (u * fall[length - 1 :]).astype(BF16)
    v_ref[...] = v.astype(BF16)
    part = dot(ys, xs, NT)
    inner = step % per_group

    @pl.when(inner == 0)
    def _():
        acc_ref[...] = part

    @pl.when(inner > 0)
    def _():
        acc_ref[...] += part

    @pl.when(inner == per_group - 1)
    def _():
        lower = iota(square, 0) >= iota(square, 1)
        upper = iota(square, 0) <= iota(square, 1)
        low_ref[...] = jnp.where(lower, dot(c, b, NT), 0.0).astype(BF16)
        up_ref[...] = jnp.where(upper, dot(b, c, NT), 0.0).astype(BF16)
        high, low = split(jnp.where(lower, acc_ref[...], 0.0), 2)
        gc_ref[...] = dot(high, b) + dot(low, b)
        gb_ref[...] = dot(high, c, ((0,), (0,))) + dot(low, c, ((0,), (0,)))


def local_part(x, dy, delta, rate, writer, reader, first_group, local_groups):
    length, lanes = x.shape
    steps = lanes // TILE
    per_group = steps // local_groups
    tile = lambda rows: pl.BlockSpec((rows, TILE), lambda i, f: (0, i))
    whole = lambda *shape: pl.BlockSpec(shape, lambda i, f: (0,) * len(shape))
    group = lambda rows, cols: pl.BlockSpec((None, rows, cols), lambda i, f: (i // per_group, 0, 0))
    proj = pl.BlockSpec((length, N), lambda i, f: (0, f[0] + i // per_group))
    shape = jax.ShapeDtypeStruct
    return pl.pallas_call(
        functools.partial(local_kernel, per_group),
        grid_spec=pltpu.PrefetchScalarGridSpec(
            num_scalar_prefetch=1,
            grid=(steps,),
            in_specs=[
                tile(length),
                tile(length),
                whole(SLOTS, length),
                whole(1, SLOTS),
                proj,
                proj,
            ],
            out_specs=[
                tile(N),
                tile(N),
                tile(length),
                tile(length),
                whole(2, length, 2 * SLOTS),
                group(length, length),
                group(length, length),
                group(length, N),
                group(length, N),
            ],
            scratch_shapes=[pltpu.VMEM((length, length), F32)],
        ),
        out_shape=[
            shape((N, lanes), BF16),
            shape((N, lanes), BF16),
            shape((length, lanes), BF16),
            shape((length, lanes), BF16),
            shape((2, length, 2 * SLOTS), BF16),
            shape((local_groups, length, length), BF16),
            shape((local_groups, length, length), BF16),
            shape((local_groups, length, N), F32),
            shape((local_groups, length, N), F32),
        ],
        cost_estimate=pl.CostEstimate(
            flops=8 * length * lanes * length, transcendentals=0, bytes_accessed=12 * length * lanes
        ),
        name="local_part",
    )(first_group, x, dy, delta, rate, writer, reader)


def final_kernel(
    per_group,
    steps,
    _,
    x_ref,
    dy_ref,
    xs_ref,
    ys_ref,
    start_ref,
    end_ref,
    u_ref,
    table_ref,
    low_ref,
    up_ref,
    b_ref,
    c_ref,
    gb_in,
    gc_in,
    skip_ref,
    delta_ref,
    rate_ref,
    out_ref,
    dx_ref,
    gb_ref,
    gc_ref,
    dd_ref,
    sums_ref,
    accb_ref,
    accc_ref,
):
    step = pl.program_id(0)
    length = x_ref.shape[0]
    lanes = spread(step)
    fall = dot(table_ref[0], lanes)
    grow = dot(table_ref[1], lanes)
    xs, ys, start = xs_ref[...], ys_ref[...], start_ref[...]
    total = fall[length - 1 :]
    end = end_ref[...].astype(F32) * total
    end_high, end_low = split(end, 2)
    core = dot(low_ref[...], xs) + dot(c_ref[...], start)
    grad = dot(up_ref[...], ys) + dot(b_ref[...], end_high) + dot(b_ref[...], end_low)
    skip = skip_ref[...]
    out_ref[...] = (fall * core + skip * x_ref[...].astype(F32)).astype(out_ref.dtype)
    dx_ref[...] = (grow * grad + skip * dy_ref[...].astype(F32)).astype(dx_ref.dtype)

    inner = step % per_group

    @pl.when(inner == 0)
    def _():
        accb_ref[...] = gb_in[...]
        accc_ref[...] = gc_in[...]

    accc_ref[...] += dot(ys, start, NT)
    accb_ref[...] += dot(xs, end_high, NT) + dot(xs, end_low, NT)

    @pl.when(inner == per_group - 1)
    def _():
        gb_ref[...] = accb_ref[...].astype(gb_ref.dtype)
        gc_ref[...] = accc_ref[...].astype(gc_ref.dtype)

    direct = xs.astype(F32) * grad
    through = ys.astype(F32) * core - direct
    shape = (TILE, 2 * SLOTS)
    column = iota(shape, 1)
    head = step * (TILE // P_SIZE) + iota(shape, 0) // P_SIZE
    pick_through = onehot(column == head)
    pick_direct = onehot(column == head + SLOTS)
    high, low = split(through, 2)
    dhigh, dlow = split(direct, 2)
    rows = dot(high, pick_through) + dot(low, pick_through)
    rows = rows + dot(dhigh, pick_direct) + dot(dlow, pick_direct)

    @pl.when(step == 0)
    def _():
        sums_ref[...] = rows

    @pl.when(step > 0)
    def _():
        sums_ref[...] += rows

    held = u_ref[...].astype(F32) / total + start.astype(F32)
    last = jnp.sum(end * held, axis=0, keepdims=True)
    at_last = jnp.where(iota((8, TILE), 0) == 7, last, 0.0)
    high, low = split(at_last, 2)
    sums_ref[length - 8 :, :] += dot(high, pick_through) + dot(low, pick_through)

    @pl.when(step == steps - 1)
    def _():
        both = sums_ref[...].T
        square = (length, length)
        later = onehot(iota(square, 0) >= iota(square, 1))
        back = sum(dot(piece, later) for piece in split(both[:SLOTS], 3))
        dd_ref[...] = both[SLOTS:] / delta_ref[...] - rate_ref[...] * back


def final_part(
    x, dy, xs, ys, start, end, u, table, low, up, gb, gc, skip, delta, rate, writer, reader, first_group, grad_dtype
):
    length, lanes = x.shape
    steps = lanes // TILE
    local_groups = low.shape[0]
    per_group = steps // local_groups
    tile = lambda rows: pl.BlockSpec((rows, TILE), lambda i, f: (0, i))
    whole = lambda *shape: pl.BlockSpec(shape, lambda i, f: (0,) * len(shape))
    group = lambda rows, cols: pl.BlockSpec((None, rows, cols), lambda i, f: (i // per_group, 0, 0))
    proj = pl.BlockSpec((length, N), lambda i, f: (0, f[0] + i // per_group))
    shape = jax.ShapeDtypeStruct
    return pl.pallas_call(
        functools.partial(final_kernel, per_group, steps),
        grid_spec=pltpu.PrefetchScalarGridSpec(
            num_scalar_prefetch=1,
            grid=(steps,),
            in_specs=[
                tile(length),
                tile(length),
                tile(length),
                tile(length),
                tile(N),
                tile(N),
                tile(N),
                whole(2, length, 2 * SLOTS),
                group(length, length),
                group(length, length),
                proj,
                proj,
                group(length, N),
                group(length, N),
                tile(1),
                whole(SLOTS, length),
                whole(SLOTS, 1),
            ],
            out_specs=[
                tile(length),
                tile(length),
                pl.BlockSpec((length, N), lambda i, f: (0, i // per_group)),
                pl.BlockSpec((length, N), lambda i, f: (0, i // per_group)),
                whole(SLOTS, length),
            ],
            scratch_shapes=[
                pltpu.VMEM((length, 2 * SLOTS), F32),
                pltpu.VMEM((length, N), F32),
                pltpu.VMEM((length, N), F32),
            ],
        ),
        out_shape=[
            shape((length, lanes), BF16),
            shape((length, lanes), BF16),
            shape((length, local_groups * N), grad_dtype),
            shape((length, local_groups * N), grad_dtype),
            shape((SLOTS, length), F32),
        ],
        cost_estimate=pl.CostEstimate(
            flops=12 * length * lanes * length, transcendentals=0, bytes_accessed=16 * length * lanes
        ),
        name="final_part",
    )(
        first_group, x, dy, xs, ys, start, end, u, table, low, up, writer, reader, gb, gc, skip, delta, rate
    )


def tree_states(u, v, decay, parents, levels):
    segs = lax.axis_size("seg")
    lanes = u.shape[1]
    chunk = lanes // segs

    def spread_heads(state):
        parts = jnp.swapaxes(state.reshape(N, segs, chunk), 0, 1)
        return lax.all_to_all(parts, "seg", 0, 0)

    decay_all = lax.all_to_all(decay.reshape(segs, chunk), "seg", 0, 0)[:, None, :]
    u_all = spread_heads(u)
    v_all = spread_heads(v).astype(F32)
    safe = jnp.maximum(parents, 0)
    starts = jnp.zeros_like(u_all)
    for repeat in range(DEPTH - 1):
        ends = (decay_all * starts.astype(F32) + u_all.astype(F32)).astype(BF16)
        starts = jnp.where((levels == repeat + 1)[:, None, None], ends[safe], starts)
    link = (parents[None, :] == jnp.arange(segs)[:, None]).astype(F32)
    grad_end = jnp.zeros_like(v_all)
    for _ in range(DEPTH - 1):
        lifted = decay_all * grad_end + v_all
        grad_end = sum(link[:, c, None, None] * lifted[c][None] for c in range(segs))

    def gather_heads(state):
        parts = lax.all_to_all(state, "seg", 0, 0)
        return jnp.swapaxes(parts, 0, 1).reshape(N, lanes)

    return gather_heads(starts), gather_heads(grad_end.astype(BF16))


def group_grads(gb, gc, members):
    shards_ = lax.axis_size("head")
    both = jnp.stack([gb, gc])
    length, width = gb.shape
    parts = both.reshape(2, shards_, length // shards_, width)
    parts = lax.all_to_all(parts, "head", 1, 1)
    if members > 1:
        parts = parts.reshape(2, shards_ // members, members, length // shards_, width).sum(2)
    parts = jnp.swapaxes(parts, 1, 2).reshape(2, length // shards_, -1)
    return parts.astype(BF16)


def chunk_of(place, k):
    return jnp.bitwise_xor(place[1], k)


def group_of(chunk, segs):
    return chunk * 2 // segs


def message_rows(width):
    return 2 * N * (width // LANES // PIECES) + EXTRA


def pack_states(ref, block, top, bottom):
    row = 2 * N * block
    ref[row : row + N, :] = top
    ref[row + N : row + 2 * N, :] = bottom


def tail_rows(rows_of):
    rows = iota((EXTRA, LANES), 0)
    tail = jnp.zeros((EXTRA, LANES), F32)
    for block, row in rows_of:
        for piece, value in enumerate(split(row, 3)):
            tail = tail + jnp.where(rows == 3 * block + piece, value.astype(F32), 0.0)
    return tail


def tail_row(tail, block):
    rows = iota((EXTRA, LANES), 0)
    own = (rows >= 3 * block) & (rows < 3 * block + 3)
    return jnp.sum(jnp.where(own, tail.astype(F32), 0.0), axis=0, keepdims=True)


def tables(delta_ref, rate_ref):
    length = delta_ref.shape[1]
    square = (length, length)
    tri = onehot(iota(square, 0) >= iota(square, 1))
    eye = onehot(iota(square, 0) == iota(square, 1))
    pieces = split(delta_ref[...], 3)
    sums = sum(dot(tri, piece, NT) for piece in pieces)
    delta = sum(dot(eye, piece, NT) for piece in pieces)
    log = rate_ref[...] * sums
    grow = split(jnp.exp(log) * delta, 2)
    fall = split(jnp.exp(-log), 2)
    return jnp.concatenate(fall, axis=1), jnp.concatenate(grow, axis=1)


def spread_at(lane):
    shape = (2 * SLOTS, TILE)
    head = (lane + iota(shape, 1)) // P_SIZE
    return onehot((iota(shape, 0) % SLOTS) == head)


def states_kernel(first, lead, place, x_ref, dy_ref, *refs):
    if lead:
        delta_ref, rate_ref, b_ref, c_ref, *outs = refs
        *messages, xs_ref, ys_ref, table_ref, bt_ref, ct_ref = outs
    else:
        table_ref, b_ref, c_ref, *outs = refs
        *messages, xs_ref, ys_ref, bt_ref, ct_ref = outs
    step = pl.program_id(0)
    length, width = x_ref.shape

    @pl.when(step == 0)
    def _():
        if lead:
            table_ref[0], table_ref[1] = tables(delta_ref, rate_ref)
        bt_ref[...] = b_ref[...].T
        ct_ref[...] = c_ref[...].T

    chunk = chunk_of(place, step + first)
    made = []
    for at in range(0, width, TILE):
        cols = slice(at, at + TILE)
        lanes = spread_at(chunk * width + at)
        fall = dot(table_ref[0], lanes)
        grow = dot(table_ref[1], lanes)
        xs, xs_low = split(x_ref[:, cols].astype(F32) * grow, 2)
        ys, ys_low = split(dy_ref[:, cols].astype(F32) * fall, 2)
        xs_ref[:, cols] = xs
        ys_ref[:, cols] = ys
        total = fall[length - 1 :]
        u = (dot(bt_ref[...], xs) + dot(bt_ref[...], xs_low)) * total
        v = dot(ct_ref[...], ys) + dot(ct_ref[...], ys_low)
        for part in range(0, TILE, LANES):
            lane = slice(part, part + LANES)
            made.append((u[:, lane].astype(BF16), v[:, lane].astype(BF16), total[:, lane]))
    for at, message in enumerate(messages):

        @pl.when(step == at // PIECES)
        def _(message=message, piece=at % PIECES):
            blocks = len(made) // PIECES
            held = made[piece * blocks : (piece + 1) * blocks]
            for block, (u, v, _) in enumerate(held):
                pack_states(message, block, u, v)
            tail = tail_rows([(block, row) for block, (_, _, row) in enumerate(held)])
            message[message.shape[0] - EXTRA :, :] = tail.astype(BF16)


def part_specs(length, width, segs, first):
    tile = lambda rows: pl.BlockSpec((rows, width), lambda i, f: (0, chunk_of(f, first + i)))
    turn = lambda rows: pl.BlockSpec((rows, width), lambda i, f: (0, i))
    whole = lambda *shape: pl.BlockSpec(shape, lambda i, f: (0,) * len(shape))
    proj = pl.BlockSpec(
        (length, N), lambda i, f: (0, 2 * f[0] + group_of(chunk_of(f, first), segs))
    )
    return tile, turn, whole, proj


def states_part(first, count, segs, place, x, dy, given, writer, reader):
    length, lanes = x.shape
    width = lanes // segs
    lead = len(given) == 2
    tile, turn, whole, proj = part_specs(length, width, segs, first)
    shape = jax.ShapeDtypeStruct
    message = shape((message_rows(width), LANES), BF16)
    scaled = shape((length, count * width), BF16)
    table = shape((2, length, 2 * SLOTS), BF16)
    return pl.pallas_call(
        functools.partial(states_kernel, first, lead),
        grid_spec=pltpu.PrefetchScalarGridSpec(
            num_scalar_prefetch=1,
            grid=(count,),
            in_specs=[tile(length), tile(length)]
            + [whole(*value.shape) for value in given]
            + [proj, proj],
            out_specs=[whole(*message.shape)] * (count * PIECES)
            + [turn(length), turn(length)]
            + ([whole(*table.shape)] if lead else []),
            scratch_shapes=[pltpu.VMEM((N, length), BF16)] * 2,
        ),
        out_shape=[message] * (count * PIECES) + [scaled, scaled] + ([table] if lead else []),
        cost_estimate=pl.CostEstimate(
            flops=8 * length * count * width * length,
            transcendentals=0,
            bytes_accessed=16 * length * count * width,
        ),
    )(place, x, dy, *given, writer, reader)


def scores_kernel(count, pairs, _, *refs):
    scaled, (b_ref, c_ref) = refs[: 2 * pairs], refs[2 * pairs : 2 * pairs + 2]
    low_ref, up_ref, gb_ref, gc_ref, acc_ref = refs[2 * pairs + 2 :]
    step = pl.program_id(0)
    length = b_ref.shape[0]
    square = (length, length)
    part = sum(dot(scaled[2 * i + 1][...], scaled[2 * i][...], NT) for i in range(pairs))

    @pl.when(step == 0)
    def _():
        acc_ref[...] = part

    @pl.when(step > 0)
    def _():
        acc_ref[...] += part

    @pl.when(step == count - 1)
    def _():
        b, c = b_ref[...], c_ref[...]
        lower = iota(square, 0) >= iota(square, 1)
        upper = iota(square, 0) <= iota(square, 1)
        low_ref[...] = jnp.where(lower, dot(c, b, NT), 0.0).astype(BF16)
        up_ref[...] = jnp.where(upper, dot(b, c, NT), 0.0).astype(BF16)
        high, low = split(jnp.where(lower, acc_ref[...], 0.0), 2)
        gc_ref[...] = dot(high, b) + dot(low, b)
        gb_ref[...] = dot(high, c, ((0,), (0,))) + dot(low, c, ((0,), (0,)))


def scores_part(first, segs, width, place, scaled, writer, reader):
    length, lanes = scaled[0].shape
    count = lanes // width
    _, turn, whole, proj = part_specs(length, width, segs, first)
    shape = jax.ShapeDtypeStruct
    return pl.pallas_call(
        functools.partial(scores_kernel, count, len(scaled) // 2),
        grid_spec=pltpu.PrefetchScalarGridSpec(
            num_scalar_prefetch=1,
            grid=(count,),
            in_specs=[turn(length)] * len(scaled) + [proj, proj],
            out_specs=[whole(length, length)] * 2 + [whole(length, N)] * 2,
            scratch_shapes=[pltpu.VMEM((length, length), F32)],
        ),
        out_shape=[shape((length, length), BF16)] * 2 + [shape((length, N), F32)] * 2,
        cost_estimate=pl.CostEstimate(
            flops=4 * length * lanes * length, transcendentals=0, bytes_accessed=8 * length * lanes
        ),
    )(place, *scaled, writer, reader)


def tree_kernel(segs, place, parents, *refs):
    got, tails = refs[:segs], refs[segs : 2 * segs]
    sent = refs[2 * segs : 3 * segs]
    all_ref, end_ref, decay_ref, tail_ref = refs[3 * segs :]
    block = pl.program_id(0)
    for k in range(segs):
        seg = chunk_of(place, k)
        all_ref[seg] = got[k][...]
        decay_ref[seg] = tail_row(tails[k][...], block)
    end_ref[...] = jnp.zeros_like(end_ref)

    for seg in range(segs):
        parent = parents[seg]
        near = jnp.maximum(parent, 0)
        above = jnp.where(parent >= 0, parents[near], -1)

        @pl.when(parent >= 0)
        def _():
            end_ref[near] += all_ref[seg, N:, :].astype(F32)

        @pl.when(above >= 0)
        def _():
            end_ref[jnp.maximum(above, 0)] += decay_ref[near] * all_ref[seg, N:, :].astype(F32)

    rows = iota((EXTRA, LANES), 0)
    for k in range(segs):
        seg = chunk_of(place, k)
        parent = parents[seg]
        near = jnp.maximum(parent, 0)
        above = jnp.where(parent >= 0, parents[near], -1)
        state = all_ref[near, :N, :].astype(F32)
        lifted = decay_ref[near] * all_ref[jnp.maximum(above, 0), :N, :].astype(F32)
        start = jnp.where(parent >= 0, state, 0.0) + jnp.where(above >= 0, lifted, 0.0)
        start = start.astype(BF16)
        own = decay_ref[seg]
        end = (own * end_ref[seg]).astype(BF16)
        held = start.astype(F32) + all_ref[seg, :N, :].astype(F32) / own
        last = jnp.sum(end.astype(F32) * held, axis=0, keepdims=True)
        at = pl.multiple_of(block * 2 * N, 2 * N)
        sent[k][pl.ds(at, N), :] = start
        sent[k][pl.ds(pl.multiple_of(at + N, N), N), :] = end
        tail = tail_rows([(block, last)])
        tail_ref[k] = jnp.where(block == 0, tail, tail_ref[k] + tail)

    @pl.when(block == pl.num_programs(0) - 1)
    def _():
        for k in range(segs):
            sent[k][sent[k].shape[0] - EXTRA :, :] = tail_ref[k].astype(BF16)


def tree_chunk(segs, place, parents, messages):
    rows, _ = messages[0].shape
    blocks = (rows - EXTRA) // (2 * N)
    state = pl.BlockSpec((2 * N, LANES), lambda i, f, p: (i, 0))
    tail = pl.BlockSpec((EXTRA, LANES), lambda i, f, p: (2 * N * blocks // EXTRA, 0))
    return pl.pallas_call(
        functools.partial(tree_kernel, segs),
        grid_spec=pltpu.PrefetchScalarGridSpec(
            num_scalar_prefetch=2,
            grid=(blocks,),
            in_specs=[state] * segs + [tail] * segs,
            out_specs=[pl.BlockSpec((rows, LANES), lambda i, f, p: (0, 0))] * segs,
            scratch_shapes=[
                pltpu.VMEM((segs, 2 * N, LANES), BF16),
                pltpu.VMEM((segs, N, LANES), F32),
                pltpu.VMEM((segs, 1, LANES), F32),
                pltpu.VMEM((segs, EXTRA, LANES), F32),
            ],
        ),
        out_shape=[jax.ShapeDtypeStruct((rows, LANES), BF16)] * segs,
        cost_estimate=pl.CostEstimate(flops=10**7, transcendentals=0, bytes_accessed=10**7),
        name="tree",
    )(place, parents, *messages, *messages)


def unpack(messages, state_ref, last_ref):
    blocks = state_ref.shape[1] // LANES // PIECES
    for piece, message in enumerate(messages):
        tail = message[2 * N * blocks :, :]
        for block in range(blocks):
            lane = (piece * blocks + block) * LANES
            cols = slice(lane, lane + LANES)
            state_ref[:, cols] = message[2 * N * block : 2 * N * (block + 1), :]
            if last_ref is not None:
                last_ref[:, cols] = tail_row(tail, block)


def hand_out(place, outs, accb_ref, accc_ref):
    block = accb_ref.shape[0] // len(outs)
    for k, out in enumerate(outs):
        row = jnp.bitwise_xor(place[0], k) * block
        rows = pl.ds(pl.multiple_of(row, block), block)
        out[0] = accb_ref[rows, :].astype(BF16)
        out[1] = accc_ref[rows, :].astype(BF16)


def grads_kernel(count, whole, place, *refs):
    messages, refs = refs[: count * PIECES], refs[count * PIECES :]
    xs_ref, ys_ref, gb_in, gc_in, *outs, accb_ref, accc_ref, state_ref = refs
    step = pl.program_id(0)

    @pl.when(step == 0)
    def _():
        accb_ref[...] = gb_in[...]
        accc_ref[...] = gc_in[...]

    for at in range(count):

        @pl.when(step == at)
        def _(parts=messages[at * PIECES : (at + 1) * PIECES]):
            unpack(parts, state_ref, None)

    accc_ref[...] += dot(ys_ref[...], state_ref[:N, :], NT)
    accb_ref[...] += dot(xs_ref[...], state_ref[N:, :], NT)

    @pl.when(step == count - 1)
    def _():
        if whole:
            outs[0][...] = accb_ref[...]
            outs[1][...] = accc_ref[...]
        else:
            hand_out(place, outs, accb_ref, accc_ref)


def grads_part(first, segs, width, heads, place, messages, xs, ys, gb, gc):
    length, lanes = xs.shape
    count = lanes // width
    _, turn, whole, _ = part_specs(length, width, segs, first)
    block = jax.ShapeDtypeStruct((2, length // max(heads, 1), N), BF16)
    total = jax.ShapeDtypeStruct((length, N), F32)
    outs = [block] * heads if heads else [total, total]
    return pl.pallas_call(
        functools.partial(grads_kernel, count, not heads),
        grid_spec=pltpu.PrefetchScalarGridSpec(
            num_scalar_prefetch=1,
            grid=(count,),
            in_specs=[whole(*messages[0].shape)] * len(messages)
            + [turn(length)] * 2
            + [whole(length, N)] * 2,
            out_specs=[whole(*out.shape) for out in outs],
            scratch_shapes=[pltpu.VMEM((length, N), F32)] * 2 + [pltpu.VMEM((2 * N, width), BF16)],
        ),
        out_shape=outs,
        cost_estimate=pl.CostEstimate(
            flops=4 * length * count * width * N,
            transcendentals=0,
            bytes_accessed=8 * length * count * width,
        ),
    )(place, *messages, xs, ys, gb, gc)


def outputs_kernel(first, count, earlier, final, place, *refs):
    messages, refs = refs[: count * PIECES], refs[count * PIECES :]
    x_ref, dy_ref, xs_ref, ys_ref, table_ref, low_ref, up_ref, b_ref, c_ref, skip_ref = refs[:10]
    refs = refs[10:]
    if earlier:
        sums_in, _, _, *refs = refs
    if final:
        delta_ref, rate_ref, gb_in, gc_in, out_ref, dx_ref, dd_ref, *refs = refs
        *outs, accb_ref, accc_ref, sums_ref, state_ref, last_ref = refs
    else:
        out_ref, dx_ref, sums_ref, state_ref, last_ref = refs
    step = pl.program_id(0)
    length, width = x_ref.shape
    for at in range(count):

        @pl.when(step == at)
        def _(parts=messages[at * PIECES : (at + 1) * PIECES]):
            unpack(parts, state_ref, last_ref)

    @pl.when(step == 0)
    def _():
        if final:
            accb_ref[...] = gb_in[...]
            accc_ref[...] = gc_in[...]
        sums_ref[...] = sums_in[...] if earlier else jnp.zeros_like(sums_ref)

    chunk = chunk_of(place, step + first)
    for at in range(0, width, TILE):
        cols = slice(at, at + TILE)
        lane = chunk * width + at
        lanes = spread_at(lane)
        fall = dot(table_ref[0], lanes)
        grow = dot(table_ref[1], lanes)
        xs, ys = xs_ref[:, cols], ys_ref[:, cols]
        start, end = state_ref[:N, cols], state_ref[N:, cols]
        core = dot(low_ref[...], xs) + dot(c_ref[...], start)
        grad = dot(up_ref[...], ys) + dot(b_ref[...], end)
        skip = skip_ref[:, cols]
        out_ref[:, cols] = (fall * core + skip * x_ref[:, cols].astype(F32)).astype(BF16)
        dx_ref[:, cols] = (grow * grad + skip * dy_ref[:, cols].astype(F32)).astype(BF16)
        if final:
            accc_ref[...] += dot(ys, start, NT)
            accb_ref[...] += dot(xs, end, NT)
        direct = xs.astype(F32) * grad
        through = ys.astype(F32) * core - direct
        shape = (TILE, 2 * SLOTS)
        column = iota(shape, 1)
        head = (lane + iota(shape, 0)) // P_SIZE
        pick_through = onehot(column == head)
        pick_direct = onehot(column == head + SLOTS)
        high, low = split(through, 2)
        dhigh, dlow = split(direct, 2)
        rows = dot(high, pick_through) + dot(low, pick_through)
        sums_ref[...] += rows + dot(dhigh, pick_direct) + dot(dlow, pick_direct)
        at_last = jnp.where(iota((8, TILE), 0) == 7, last_ref[:, cols], 0.0)
        high, low = split(at_last, 2)
        sums_ref[length - 8 :, :] += dot(high, pick_through) + dot(low, pick_through)

    if final:

        @pl.when(step == count - 1)
        def _():
            hand_out(place, outs, accb_ref, accc_ref)
            both = sums_ref[...].T
            square = (length, length)
            later = onehot(iota(square, 0) >= iota(square, 1))
            back = sum(dot(piece, later) for piece in split(both[:SLOTS], 3))
            dd_ref[...] = both[SLOTS:] / delta_ref[...] - rate_ref[...] * back


def outputs_part(first, segs, place, messages, x, dy, xs, ys, table, low, up, skip, writer, reader, earlier=(), final=(), heads=0):
    length, lanes = x.shape
    width = lanes // segs
    count = len(messages) // PIECES
    tile, turn, whole, proj = part_specs(length, width, segs, first)
    shape = jax.ShapeDtypeStruct
    sums = shape((length, 2 * SLOTS), F32)
    full = shape((length, lanes), BF16)
    any_ = pl.BlockSpec(memory_space=pl.ANY)
    in_specs = (
        [whole(*messages[0].shape)] * len(messages)
        + [tile(length), tile(length), turn(length), turn(length)]
        + [whole(*table.shape), whole(length, length), whole(length, length), proj, proj]
        + [tile(1)]
    )
    args = [*messages, x, dy, xs, ys, table, low, up, writer, reader, skip]
    aliases = {}
    if earlier:
        in_specs += [whole(*sums.shape), any_, any_]
        args += list(earlier)
        aliases = {len(args) - 1: 0, len(args): 1}
    in_specs += [whole(*value.shape) for value in final]
    args += list(final)
    scratch = [pltpu.VMEM((2 * N, width), BF16), pltpu.VMEM((1, width), F32)]
    out_specs, out_shape = [tile(length), tile(length)], [full, full]
    if final:
        delta = final[0]
        out_specs.append(whole(*delta.shape))
        out_shape.append(shape(delta.shape, F32))
        block = shape((2, length // heads, N), BF16)
        out_specs += [whole(*block.shape)] * heads
        out_shape += [block] * heads
        scratch = [pltpu.VMEM((length, N), F32)] * 2 + [pltpu.VMEM(sums.shape, F32)] + scratch
    else:
        out_specs.append(whole(*sums.shape))
        out_shape.append(sums)
    return pl.pallas_call(
        functools.partial(outputs_kernel, first, count, bool(earlier), bool(final)),
        grid_spec=pltpu.PrefetchScalarGridSpec(
            num_scalar_prefetch=1,
            grid=(count,),
            in_specs=in_specs,
            out_specs=out_specs,
            scratch_shapes=scratch,
        ),
        out_shape=out_shape,
        input_output_aliases=aliases,
        cost_estimate=pl.CostEstimate(
            flops=12 * length * count * width * length,
            transcendentals=0,
            bytes_accessed=16 * length * count * width,
        ),
    )(place, *args)


def place_kernel(heads, segs, place, *refs):
    near, far, (gb_ref, gc_ref) = refs[:heads], refs[heads : 2 * heads], refs[2 * heads :]
    for k in range(heads):
        owner = jnp.bitwise_xor(place[0], k)
        for half, parts in enumerate((near, far)):
            group = 2 * owner + group_of(chunk_of(place, half * segs // 2), segs)
            cols = pl.ds(pl.multiple_of(group * N, N), N)
            gb_ref[:, cols] = parts[k][0]
            gc_ref[:, cols] = parts[k][1]


def place_grads(segs, place, near, far):
    heads = len(near)
    rows = near[0].shape[1]
    shape = jax.ShapeDtypeStruct((rows, 2 * heads * N), BF16)
    return pl.pallas_call(
        functools.partial(place_kernel, heads, segs),
        grid_spec=pltpu.PrefetchScalarGridSpec(
            num_scalar_prefetch=1,
            grid=(1,),
            in_specs=[pl.BlockSpec(near[0].shape, lambda i, f: (0, 0, 0))] * (2 * heads),
            out_specs=[pl.BlockSpec(shape.shape, lambda i, f: (0, 0))] * 2,
        ),
        out_shape=[shape] * 2,
        name="place_grads",
    )(place, *near, *far)


def swap(value, axis, k):
    size = lax.axis_size(axis)
    return lax.ppermute(value, axis, [(i, i ^ k) for i in range(size)])


def paired(inputs, deltas, rates, skips, writer, reader, grad_out, parents):
    segs = lax.axis_size("seg")
    heads = lax.axis_size("head")
    mid, late = segs // 2, 3 * segs // 4
    near_ks, mid_ks, late_ks = range(mid), range(mid, late), range(late, segs)
    place = jnp.stack([lax.axis_index("head"), lax.axis_index("seg")]).astype(jnp.int32)
    x, dy, b, c = inputs[0], grad_out[0], writer[0], reader[0]
    width = x.shape[1] // segs
    delta = deltas[0]
    own, got, back = {}, {}, {}

    def keep(ks, messages):
        for at, message in enumerate(messages):
            own[ks[at // PIECES], at % PIECES] = message

    def move(out, values, ks, piece):
        for k in ks:
            out[k, piece] = swap(values[k, piece], "seg", k) if k else values[k, piece]

    def arrived(ks):
        return [back[k, piece] for k in ks for piece in range(PIECES)]

    *parts, xs1, ys1, table = states_part(
        mid, late - mid, segs, place, x, dy, (delta, rates[None, :]), b, c
    )
    keep(mid_ks, parts)
    move(got, own, mid_ks, 0)
    *parts, xs2, ys2 = states_part(late, segs - late, segs, place, x, dy, (table,), b, c)
    keep(late_ks, parts)
    move(got, own, late_ks, 0)
    *parts, xs0, ys0 = states_part(0, mid, segs, place, x, dy, (table,), b, c)
    keep(near_ks, parts)
    move(got, own, near_ks, 0)
    for piece in range(1, PIECES):
        move(got, own, mid_ks, piece)
        move(got, own, late_ks, piece)
        move(got, own, near_ks, piece)
    low1, up1, gb1, gc1 = scores_part(mid, segs, width, place, (xs1, ys1, xs2, ys2), b, c)
    low0, up0, gb0, gc0 = scores_part(0, segs, width, place, (xs0, ys0), b, c)
    for piece in range(PIECES):
        sent = tree_chunk(segs, place, parents, [got[k, piece] for k in range(segs)])
        sent = {(k, piece): value for k, value in enumerate(sent)}
        move(back, sent, near_ks, piece)
        move(back, sent, mid_ks, piece)
        move(back, sent, late_ks, piece)
    skip = jnp.repeat(skips, P_SIZE)[None, :]
    grads0 = grads_part(0, segs, width, heads, place, arrived(near_ks), xs0, ys0, gb0, gc0)
    moved0 = [grads0[0]] + [swap(grads0[k], "head", k) for k in range(1, heads)]
    common = (table, low0, up0, skip, b, c)
    out, dx, sums = outputs_part(0, segs, place, arrived(near_ks), x, dy, xs0, ys0, *common)
    common = (table, low1, up1, skip, b, c)
    gb1, gc1 = grads_part(mid, segs, width, 0, place, arrived(mid_ks), xs1, ys1, gb1, gc1)
    out, dx, sums = outputs_part(
        mid, segs, place, arrived(mid_ks), x, dy, xs1, ys1, *common, (sums, out, dx)
    )
    out, dx, dd, *grads1 = outputs_part(
        late,
        segs,
        place,
        arrived(late_ks),
        x,
        dy,
        xs2,
        ys2,
        *common,
        (sums, out, dx),
        (delta, rates[:, None], gb1, gc1),
        heads,
    )
    moved1 = [grads1[0]] + [swap(grads1[k], "head", k) for k in range(1, heads)]
    gb, gc = place_grads(segs, place, moved0, moved1)
    return out[None], dx[None], dd[None], gb[None], gc[None]


def power_of_two(size):
    return size & (size - 1) == 0


def shards(inputs, deltas, rates, skips, writer, reader, grad_out, parents, levels):
    heads = deltas.shape[1]
    per_group_all = H // G
    local_groups = max(1, heads // per_group_all)
    members = max(1, per_group_all // heads)
    segs = lax.axis_size("seg")
    lanes = inputs.shape[2]
    even = power_of_two(segs) and power_of_two(lax.axis_size("head")) and segs >= 4
    if even and local_groups == 2 and heads == SLOTS and lanes // segs % TILE == 0:
        return paired(inputs, deltas, rates, skips, writer, reader, grad_out, parents)
    first_group = (lax.axis_index("head") * heads // per_group_all).astype(jnp.int32)[None]
    x, dy = inputs[0], grad_out[0]
    pad = SLOTS - heads
    delta = jnp.pad(deltas[0], ((0, pad), (0, 0)))
    rate = jnp.pad(rates, (0, pad))
    u, v, xs, ys, table, low, up, gb, gc = local_part(
        x, dy, delta, rate[None, :], writer[0], reader[0], first_group, local_groups
    )
    decay = jnp.repeat(jnp.exp(-rates * jnp.sum(deltas[0], axis=1)), P_SIZE)
    start, end = tree_states(u, v, decay, parents, levels)
    out, dx, gb, gc, dd = final_part(
        x,
        dy,
        xs,
        ys,
        start,
        end,
        u,
        table,
        low,
        up,
        gb,
        gc,
        jnp.repeat(skips, P_SIZE)[None, :],
        delta,
        rate[:, None],
        writer[0],
        reader[0],
        first_group,
        BF16 if members == 1 else F32,
    )
    grads = group_grads(gb, gc, members)
    return (out[None], dx[None], dd[None, :heads], grads[0][None], grads[1][None])


def solution(mesh):
    placed = (
        P("seg", None, "head"),
        P("seg", "head", None),
        P("head"),
        P("head"),
        P("seg", None, None),
        P("seg", None, None),
        P("seg", None, "head"),
        P(),
        P(),
    )
    return jax.shard_map(
        shards,
        mesh=mesh,
        in_specs=placed,
        out_specs=(
            P("seg", None, "head"),
            P("seg", None, "head"),
            P("seg", "head", None),
            P("seg", "head", None),
            P("seg", "head", None),
        ),
        check_vma=False,
    )
```

profile of v0, /device:TPU:0, one launch (start us, length us, event | category | flops | bytes accessed | tf_op | source)
XLA Modules:
  0.0 156.5 jit_solution(16931493042396280537)
XLA Ops:
  1.3 4.9 %shard_map.119 = (bf16[528,128]{1,0:T(8,128)(2,1)}, bf16[528,128]{1,0:T(8,128)(2,1)}, bf16[528,128]{1,0:T(8,128)(2,1)}, bf16[528,128]{1,0:T(8,128)(2,1)}, bf16[2...) custom-call(s32[2]{0:T(128)} %pad_add_fusion.place._, bf16[256,4096]{1,0:T(8,128)(2,1)} %bitcast.14, ...), custom_call_target="tpu_custom_call" | custom-call | flops 536870912 | bytes 4194304 | tf_op jit(solution)/shard_map/pallas_call | solution.py:500
  6.2 6.8 %shard_map.120 = (bf16[528,128]{1,0:T(8,128)(2,1)}, bf16[528,128]{1,0:T(8,128)(2,1)}, bf16[528,128]{1,0:T(8,128)(2,1)}, bf16[528,128]{1,0:T(8,128)(2,1)}, bf16[5...) custom-call(s32[2]{0:T(128)} %pad_add_fusion.place._, ...), custom_call_target="tpu_custom_call" | custom-call | flops 1073741824 | bytes 8388608 | tf_op jit(solution)/shard_map/pallas_call | solution.py:500
  13.0 2.5 %collective-permute-start.10 = (bf16[528,128]{1,0:T(8,128)(2,1)}, bf16[528,128]{1,0:T(8,128)(2,1)S(1)}, u32[]{:S(2)}, u32[]{:S(2)}) collective-permute-start(bf16[528,128]{1,0:T(8,128)(2,1)} %get-tuple-element.86), channel_id=1, source_target_pairs={{0,12},{4,8},{8,4},{12,0},{16,28},{20,24},{24,20},{28,16},{1,13},{... | collective-permute-start | bytes 405512 | tf_op jit(solution)/shard_map/ppermute | solution.py:877
  16.3 4.7 %shard_map.121 = (bf16[528,128]{1,0:T(8,128)(2,1)}, bf16[528,128]{1,0:T(8,128)(2,1)}, bf16[528,128]{1,0:T(8,128)(2,1)}, bf16[528,128]{1,0:T(8,128)(2,1)}, bf16[2...) custom-call(s32[2]{0:T(128)} %pad_add_fusion.place._, bf16[256,4096]{1,0:T(8,128)(2,1)} %bitcast.16, ...), custom_call_target="tpu_custom_call" | custom-call | flops 536870912 | bytes 4194304 | tf_op jit(solution)/shard_map/pallas_call | solution.py:500
  21.0 3.9 %collective-permute-start.13 = (bf16[528,128]{1,0:T(8,128)(2,1)}, bf16[528,128]{1,0:T(8,128)(2,1)S(1)}, u32[]{:S(2)}, u32[]{:S(2)}) collective-permute-start(bf16[528,128]{1,0:T(8,128)(2,1)} %get-tuple-element.89), channel_id=1, source_target_pairs={{0,24},{4,28},{8,16},{12,20},{16,8},{20,12},{24,0},{28,4},{1,25},{... | collective-permute-start | bytes 405512 | tf_op jit(solution)/shard_map/ppermute | solution.py:877
  29.2 11.7 %collective-permute-start.1 = (bf16[528,128]{1,0:T(8,128)(2,1)S(1)}, bf16[528,128]{1,0:T(8,128)(2,1)S(1)}, u32[]{:S(2)}, u32[]{:S(2)}) collective-permute-start(bf16[528,128]{1,0:T(8,128)(2,1)S(1)} %copy-done.46), channel_id=1, source_target_pairs={{0,8},{4,12},{8,0},{12,4},{16,24},{20,28},{24,16},{28,20},{1,9},{5... | collective-permute-start | bytes 405512 | tf_op jit(solution)/shard_map/ppermute | solution.py:877
  43.3 3.0 %collective-permute-done.11.refs_4_.refs_12_ = bf16[528,128]{1,0:T(8,128)(2,1)S(1)} collective-permute-done((bf16[528,128]{1,0:T(8,128)(2,1)S(1)}, bf16[528,128]{1,0:T(8,128)(2,1)S(1)}, u32[]{:S(2)}, u32[]{:S(2)}) %collective-permute-start.11) | collective-permute-done | bytes 135200 | tf_op jit(solution)/shard_map/ppermute | solution.py:877
  46.3 2.7 %collective-permute-start.5 = (bf16[528,128]{1,0:T(8,128)(2,1)}, bf16[528,128]{1,0:T(8,128)(2,1)S(1)}, u32[]{:S(2)}, u32[]{:S(2)}) collective-permute-start(bf16[528,128]{1,0:T(8,128)(2,1)} %get-tuple-element.80), channel_id=1, source_target_pairs={{0,24},{4,28},{8,16},{12,20},{16,8},{20,12},{24,0},{28,4},{1,25},{... | collective-permute-start | bytes 405512 | tf_op jit(solution)/shard_map/ppermute | solution.py:877
  49.0 3.7 %collective-permute-start.6 = (bf16[528,128]{1,0:T(8,128)(2,1)}, bf16[528,128]{1,0:T(8,128)(2,1)S(1)}, u32[]{:S(2)}, u32[]{:S(2)}) collective-permute-start(bf16[528,128]{1,0:T(8,128)(2,1)} %get-tuple-element.81), channel_id=1, source_target_pairs={{0,28},{4,24},{8,20},{12,16},{16,12},{20,8},{24,4},{28,0},{1,29},{... | collective-permute-start | bytes 405512 | tf_op jit(solution)/shard_map/ppermute | solution.py:877
  52.9 4.0 %tree.3 = (bf16[528,128]{1,0:T(8,128)(2,1)}, bf16[528,128]{1,0:T(8,128)(2,1)}, bf16[528,128]{1,0:T(8,128)(2,1)}, bf16[528,128]{1,0:T(8,128)(2,1)}, bf16[528,128]...) custom-call(s32[2]{0:T(128)} %pad_add_fusion.place._, s32[8]{0:T(128)} %parents.3, ...), custom_call_target="tpu_custom_call" | custom-call | flops 10000000 | bytes 10000000 | tf_op jit(solution)/shard_map/tree/pallas_call | solution.py:626
  57.0 3.0 %collective-permute-start.23 = (bf16[528,128]{1,0:T(8,128)(2,1)}, bf16[528,128]{1,0:T(8,128)(2,1)S(1)}, u32[]{:S(2)}, u32[]{:S(2)}) collective-permute-start(bf16[528,128]{1,0:T(8,128)(2,1)} %get-tuple-element.107), channel_id=1, source_target_pairs={{0,4},{4,0},{8,12},{12,8},{16,20},{20,16},{24,28},{28,24},{1,5},{5... | collective-permute-start | bytes 405512 | tf_op jit(solution)/shard_map/ppermute | solution.py:877
  60.0 4.1 %collective-permute-start.25 = (bf16[528,128]{1,0:T(8,128)(2,1)}, bf16[528,128]{1,0:T(8,128)(2,1)S(1)}, u32[]{:S(2)}, u32[]{:S(2)}) collective-permute-start(bf16[528,128]{1,0:T(8,128)(2,1)} %get-tuple-element.109), channel_id=1, source_target_pairs={{0,8},{4,12},{8,0},{12,4},{16,24},{20,28},{24,16},{28,20},{1,9},{5... | collective-permute-start | bytes 405512 | tf_op jit(solution)/shard_map/ppermute | solution.py:877
  66.4 3.0 %collective-permute-done.3.refs_4_.refs_12_ = bf16[528,128]{1,0:T(8,128)(2,1)S(1)} collective-permute-done((bf16[528,128]{1,0:T(8,128)(2,1)S(1)}, bf16[528,128]{1,0:T(8,128)(2,1)S(1)}, u32[]{:S(2)}, u32[]{:S(2)}) %collective-permute-start.3) | collective-permute-done | bytes 135200 | tf_op jit(solution)/shard_map/ppermute | solution.py:877
  71.1 3.9 %tree.2 = (bf16[528,128]{1,0:T(8,128)(2,1)}, bf16[528,128]{1,0:T(8,128)(2,1)}, bf16[528,128]{1,0:T(8,128)(2,1)}, bf16[528,128]{1,0:T(8,128)(2,1)}, bf16[528,128]...) custom-call(s32[2]{0:T(128)} %pad_add_fusion.place._, s32[8]{0:T(128)} %parents.3, ...), custom_call_target="tpu_custom_call" | custom-call | flops 10000000 | bytes 10000000 | tf_op jit(solution)/shard_map/tree/pallas_call | solution.py:626
  83.1 3.8 %shard_map.122 = (bf16[256,256]{1,0:T(8,128)(2,1)}, bf16[256,256]{1,0:T(8,128)(2,1)}, f32[256,128]{1,0:T(8,128)}, f32[256,128]{1,0:T(8,128)}) custom-call(s32[2]{0:T(128)} %pad_add_fusion.place._, bf16[256,1024]{1,0:T(8,128)(2,1)} %get-tuple-element.96.refs_0_.refs_6_.refs_4_, bf16[256,1024]{1,0:T(8,128)(2,1)} %get-tuple-element.97.refs_1_.refs_7_.refs_5_, ...), custom_call_target="tpu_custom_call" | custom-call | flops 268435456 | bytes 2097152 | tf_op jit(solution)/shard_map/pallas_call | solution.py:555
  87.0 5.1 %shard_map.123 = (bf16[256,256]{1,0:T(8,128)(2,1)}, bf16[256,256]{1,0:T(8,128)(2,1)}, f32[256,128]{1,0:T(8,128)}, f32[256,128]{1,0:T(8,128)}) custom-call(s32[2]{0:T(128)} %pad_add_fusion.place._, bf16[256,2048]{1,0:T(8,128)(2,1)} %get-tuple-element.112.refs_0_.refs_10_.refs_8_, bf16[256,2048]{1,0:T(8,128)(2,1)} %get-tuple-element.113.refs_1_.refs_11_.refs_9_, ...), custom_call_target="tpu_custom_call" | custom-call | flops 536870912 | bytes 4194304 | tf_op jit(solution)/shard_map/pallas_call | solution.py:555
  93.3 2.7 %collective-permute-start.15 = (bf16[528,128]{1,0:T(8,128)(2,1)S(1)}, bf16[528,128]{1,0:T(8,128)(2,1)S(1)}, u32[]{:S(2)}, u32[]{:S(2)}) collective-permute-start(bf16[528,128]{1,0:T(8,128)(2,1)S(1)} %copy-done.37), channel_id=1, source_target_pairs={{0,24},{4,28},{8,16},{12,20},{16,8},{20,12},{24,0},{28,4},{1,25},{... | collective-permute-start | bytes 405512 | tf_op jit(solution)/shard_map/ppermute | solution.py:877
  97.3 11.3 %collective-permute-start.16 = (bf16[528,128]{1,0:T(8,128)(2,1)S(1)}, bf16[528,128]{1,0:T(8,128)(2,1)S(1)}, u32[]{:S(2)}, u32[]{:S(2)}) collective-permute-start(bf16[528,128]{1,0:T(8,128)(2,1)S(1)} %copy-done.39), channel_id=1, source_target_pairs={{0,28},{4,24},{8,20},{12,16},{16,12},{20,8},{24,4},{28,0},{1,29},{... | collective-permute-start | bytes 405512 | tf_op jit(solution)/shard_map/ppermute | solution.py:877
  109.4 2.6 %collective-permute-start.7 = (bf16[528,128]{1,0:T(8,128)(2,1)S(1)}, bf16[528,128]{1,0:T(8,128)(2,1)S(1)}, u32[]{:S(2)}, u32[]{:S(2)}) collective-permute-start(bf16[528,128]{1,0:T(8,128)(2,1)S(1)} %copy-done.38), channel_id=1, source_target_pairs={{0,24},{4,28},{8,16},{12,20},{16,8},{20,12},{24,0},{28,4},{1,25},{... | collective-permute-start | bytes 405512 | tf_op jit(solution)/shard_map/ppermute | solution.py:877
  112.0 8.5 %shard_map.124 = (bf16[256,4096]{1,0:T(8,128)(2,1)}, bf16[256,4096]{1,0:T(8,128)(2,1)}, f32[256,128]{1,0:T(8,128)}) custom-call(s32[2]{0:T(128)} %pad_add_fusion.place._, bf16[528,128]{1,0:T(8,128)(2,1)} %get-tuple-element.104.refs_0_, bf16[528,128]{1,0:T(8,128)(2,1)} %get-tuple-element.105.refs_1_, bf16[528,128]{1,0:T(8,128)(2,1)} %copy-done.3, ...), custom_call_target="tpu_custom_call" | custom-call | flops 1610612736 | bytes 8388608 | tf_op jit(solution)/shard_map/pallas_call | solution.py:828
  120.6 5.0 %shard_map.128 = (bf16[2,64,128]{2,1,0:T(8,128)(2,1)}, bf16[2,64,128]{2,1,0:T(8,128)(2,1)}, bf16[2,64,128]{2,1,0:T(8,128)(2,1)}, bf16[2,64,128]{2,1,0:T(8,128)(2,1)}) custom-call(s32[2]{0:T(128)} %pad_add_fusion.place._, bf16[528,128]{1,0:T(8,128)(2,1)} %get-tuple-element.104.refs_0_, bf16[528,128]{1,0:T(8,128)(2,1)} %get-tuple-element.105.refs_1_, ...), custom_call_target="tpu_custom_call" | custom-call | flops 268435456 | bytes 4194304 | tf_op jit(solution)/shard_map/pallas_call | solution.py:702
  127.1 3.4 %shard_map.126 = (f32[256,128]{1,0:T(8,128)}, f32[256,128]{1,0:T(8,128)}) custom-call(s32[2]{0:T(128)} %pad_add_fusion.place._, bf16[528,128]{1,0:T(8,128)(2,1)} %copy-done.22, bf16[528,128]{1,0:T(8,128)(2,1)} %copy-done.20, bf16[528,128]{1,0:T(8,128)(2,1)} %copy-done.23, bf16[528,128]{1,0:T(8,128)(2,1)} %copy-done.21, ...), custom_call_target="tpu_custom_call" | custom-call | flops 134217728 | bytes 2097152 | tf_op jit(solution)/shard_map/pallas_call | solution.py:702
  130.5 5.8 %shard_map.125 = (bf16[256,4096]{1,0:T(8,128)(2,1)}, bf16[256,4096]{1,0:T(8,128)(2,1)}, f32[256,128]{1,0:T(8,128)}) custom-call(s32[2]{0:T(128)} %pad_add_fusion.place._, bf16[528,128]{1,0:T(8,128)(2,1)} %copy-done.22, bf16[528,128]{1,0:T(8,128)(2,1)} %copy-done.20, bf16[528,128]{1,0:T(8,128)(2,1)} %copy-done.23, ...), custom_call_target="tpu_custom_call", output_to_operand_aliasing={{0}: (16, {}), {1}: (17, {})} | custom-call | flops 805306368 | bytes 4194304 | tf_op jit(solution)/shard_map/pallas_call | solution.py:828
  139.2 6.3 %shard_map.127 = (bf16[256,4096]{1,0:T(8,128)(2,1)}, bf16[256,4096]{1,0:T(8,128)(2,1)}, f32[64,256]{1,0:T(8,128)}, bf16[2,64,128]{2,1,0:T(8,128)(2,1)}, bf16[2,6...) custom-call(s32[2]{0:T(128)} %pad_add_fusion.place._, ...), custom_call_target="tpu_custom_call", output_to_operand_aliasing={{0}: (16, {}), {1}: (17, {})} | custom-call | flops 805306368 | bytes 4194304 | tf_op jit(solution)/shard_map/pallas_call | solution.py:828
  (165 shorter events, 38.9 us)
Async XLA Ops:
  24.9 16.0 %collective-permute-start.14 = (bf16[528,128]{1,0:T(8,128)(2,1)}, bf16[528,128]{1,0:T(8,128)(2,1)S(1)}, u32[]{:S(2)}, u32[]{:S(2)}) collective-permute-start(bf16[528,128]{1,0:T(8,128)(2,1)} %get-tuple-element.90), channel_id=1, source_target_pairs={{0,28},{4,24},{8,20},{12,16},{16,12},{20,8},{24,4},{28,0},{1,29},{... | collective-permute-start | bytes 405512 | tf_op jit(solution)/shard_map/ppermute | solution.py:877
  24.9 21.3 %collective-permute-start.11 = (bf16[528,128]{1,0:T(8,128)(2,1)S(1)}, bf16[528,128]{1,0:T(8,128)(2,1)S(1)}, u32[]{:S(2)}, u32[]{:S(2)}) collective-permute-start(bf16[528,128]{1,0:T(8,128)(2,1)S(1)} %copy-done.49), channel_id=1, source_target_pairs={{0,16},{4,20},{8,24},{12,28},{16,0},{20,4},{24,8},{28,12},{1,17},{... | collective-permute-start | bytes 405512 | tf_op jit(solution)/shard_map/ppermute | solution.py:877
  25.2 23.7 %collective-permute-start.12 = (bf16[528,128]{1,0:T(8,128)(2,1)S(1)}, bf16[528,128]{1,0:T(8,128)(2,1)S(1)}, u32[]{:S(2)}, u32[]{:S(2)}) collective-permute-start(bf16[528,128]{1,0:T(8,128)(2,1)S(1)} %copy-done.47), channel_id=1, source_target_pairs={{0,20},{4,16},{8,28},{12,24},{16,4},{20,0},{24,12},{28,8},{1,21},{... | collective-permute-start | bytes 405512 | tf_op jit(solution)/shard_map/ppermute | solution.py:877
  27.5 25.2 %collective-permute-start = (bf16[528,128]{1,0:T(8,128)(2,1)S(1)}, bf16[528,128]{1,0:T(8,128)(2,1)S(1)}, u32[]{:S(2)}, u32[]{:S(2)}) collective-permute-start(bf16[528,128]{1,0:T(8,128)(2,1)S(1)} %copy-done.48), channel_id=1, source_target_pairs={{0,4},{4,0},{8,12},{12,8},{16,20},{20,16},{24,28},{28,24},{1,5},{5... | collective-permute-start | bytes 405512 | tf_op jit(solution)/shard_map/ppermute | solution.py:877
  29.2 23.5 %collective-permute-start.1 = (bf16[528,128]{1,0:T(8,128)(2,1)S(1)}, bf16[528,128]{1,0:T(8,128)(2,1)S(1)}, u32[]{:S(2)}, u32[]{:S(2)}) collective-permute-start(bf16[528,128]{1,0:T(8,128)(2,1)S(1)} %copy-done.46), channel_id=1, source_target_pairs={{0,8},{4,12},{8,0},{12,4},{16,24},{20,28},{24,16},{28,20},{1,9},{5... | collective-permute-start | bytes 405512 | tf_op jit(solution)/shard_map/ppermute | solution.py:877
  40.9 16.0 %collective-permute-start.2 = (bf16[528,128]{1,0:T(8,128)(2,1)S(1)}, bf16[528,128]{1,0:T(8,128)(2,1)S(1)}, u32[]{:S(2)}, u32[]{:S(2)}) collective-permute-start(bf16[528,128]{1,0:T(8,128)(2,1)S(1)} %copy-done.45), channel_id=1, source_target_pairs={{0,12},{4,8},{8,4},{12,0},{16,28},{20,24},{24,20},{28,16},{1,13},{... | collective-permute-start | bytes 405512 | tf_op jit(solution)/shard_map/ppermute | solution.py:877
  46.3 13.8 %collective-permute-start.5 = (bf16[528,128]{1,0:T(8,128)(2,1)}, bf16[528,128]{1,0:T(8,128)(2,1)S(1)}, u32[]{:S(2)}, u32[]{:S(2)}) collective-permute-start(bf16[528,128]{1,0:T(8,128)(2,1)} %get-tuple-element.80), channel_id=1, source_target_pairs={{0,24},{4,28},{8,16},{12,20},{16,8},{20,12},{24,0},{28,4},{1,25},{... | collective-permute-start | bytes 405512 | tf_op jit(solution)/shard_map/ppermute | solution.py:877
  49.0 15.1 %collective-permute-start.6 = (bf16[528,128]{1,0:T(8,128)(2,1)}, bf16[528,128]{1,0:T(8,128)(2,1)S(1)}, u32[]{:S(2)}, u32[]{:S(2)}) collective-permute-start(bf16[528,128]{1,0:T(8,128)(2,1)} %get-tuple-element.81), channel_id=1, source_target_pairs={{0,28},{4,24},{8,20},{12,16},{16,12},{20,8},{24,4},{28,0},{1,29},{... | collective-permute-start | bytes 405512 | tf_op jit(solution)/shard_map/ppermute | solution.py:877
  52.7 16.7 %collective-permute-start.3 = (bf16[528,128]{1,0:T(8,128)(2,1)S(1)}, bf16[528,128]{1,0:T(8,128)(2,1)S(1)}, u32[]{:S(2)}, u32[]{:S(2)}) collective-permute-start(bf16[528,128]{1,0:T(8,128)(2,1)S(1)} %copy-done.41), channel_id=1, source_target_pairs={{0,16},{4,20},{8,24},{12,28},{16,0},{20,4},{24,8},{28,12},{1,17},{... | collective-permute-start | bytes 405512 | tf_op jit(solution)/shard_map/ppermute | solution.py:877
  52.8 17.6 %collective-permute-start.4 = (bf16[528,128]{1,0:T(8,128)(2,1)S(1)}, bf16[528,128]{1,0:T(8,128)(2,1)S(1)}, u32[]{:S(2)}, u32[]{:S(2)}) collective-permute-start(bf16[528,128]{1,0:T(8,128)(2,1)S(1)} %copy-done.40), channel_id=1, source_target_pairs={{0,20},{4,16},{8,28},{12,24},{16,4},{20,0},{24,12},{28,8},{1,21},{... | collective-permute-start | bytes 405512 | tf_op jit(solution)/shard_map/ppermute | solution.py:877
  57.0 18.9 %collective-permute-start.23 = (bf16[528,128]{1,0:T(8,128)(2,1)}, bf16[528,128]{1,0:T(8,128)(2,1)S(1)}, u32[]{:S(2)}, u32[]{:S(2)}) collective-permute-start(bf16[528,128]{1,0:T(8,128)(2,1)} %get-tuple-element.107), channel_id=1, source_target_pairs={{0,4},{4,0},{8,12},{12,8},{16,20},{20,16},{24,28},{28,24},{1,5},{5... | collective-permute-start | bytes 405512 | tf_op jit(solution)/shard_map/ppermute | solution.py:877
  60.0 17.3 %collective-permute-start.25 = (bf16[528,128]{1,0:T(8,128)(2,1)}, bf16[528,128]{1,0:T(8,128)(2,1)S(1)}, u32[]{:S(2)}, u32[]{:S(2)}) collective-permute-start(bf16[528,128]{1,0:T(8,128)(2,1)} %get-tuple-element.109), channel_id=1, source_target_pairs={{0,8},{4,12},{8,0},{12,4},{16,24},{20,28},{24,16},{28,20},{1,9},{5... | collective-permute-start | bytes 405512 | tf_op jit(solution)/shard_map/ppermute | solution.py:877
  64.1 15.1 %collective-permute-start.27 = (bf16[528,128]{1,0:T(8,128)(2,1)}, bf16[528,128]{1,0:T(8,128)(2,1)S(1)}, u32[]{:S(2)}, u32[]{:S(2)}) collective-permute-start(bf16[528,128]{1,0:T(8,128)(2,1)} %get-tuple-element.111), channel_id=1, source_target_pairs={{0,12},{4,8},{8,4},{12,0},{16,28},{20,24},{24,20},{28,16},{1,13},{... | collective-permute-start | bytes 405512 | tf_op jit(solution)/shard_map/ppermute | solution.py:877
  75.8 16.2 %collective-permute-start.24 = (bf16[528,128]{1,0:T(8,128)(2,1)}, bf16[528,128]{1,0:T(8,128)(2,1)S(1)}, u32[]{:S(2)}, u32[]{:S(2)}) collective-permute-start(bf16[528,128]{1,0:T(8,128)(2,1)} %get-tuple-element.108), channel_id=1, source_target_pairs={{0,8},{4,12},{8,0},{12,4},{16,24},{20,28},{24,16},{28,20},{1,9},{5... | collective-permute-start | bytes 405512 | tf_op jit(solution)/shard_map/ppermute | solution.py:877
  75.8 17.4 %collective-permute-start.26 = (bf16[528,128]{1,0:T(8,128)(2,1)}, bf16[528,128]{1,0:T(8,128)(2,1)S(1)}, u32[]{:S(2)}, u32[]{:S(2)}) collective-permute-start(bf16[528,128]{1,0:T(8,128)(2,1)} %get-tuple-element.110), channel_id=1, source_target_pairs={{0,12},{4,8},{8,4},{12,0},{16,28},{20,24},{24,20},{28,16},{1,13},{... | collective-permute-start | bytes 405512 | tf_op jit(solution)/shard_map/ppermute | solution.py:877
  77.3 18.7 %collective-permute-start.19 = (bf16[528,128]{1,0:T(8,128)(2,1)S(1)}, bf16[528,128]{1,0:T(8,128)(2,1)S(1)}, u32[]{:S(2)}, u32[]{:S(2)}) collective-permute-start(bf16[528,128]{1,0:T(8,128)(2,1)S(1)} %copy-done.43), channel_id=1, source_target_pairs={{0,16},{4,20},{8,24},{12,28},{16,0},{20,4},{24,8},{28,12},{1,17},{... | collective-permute-start | bytes 405512 | tf_op jit(solution)/shard_map/ppermute | solution.py:877
  79.1 18.1 %collective-permute-start.21 = (bf16[528,128]{1,0:T(8,128)(2,1)S(1)}, bf16[528,128]{1,0:T(8,128)(2,1)S(1)}, u32[]{:S(2)}, u32[]{:S(2)}) collective-permute-start(bf16[528,128]{1,0:T(8,128)(2,1)S(1)} %copy-done.42), channel_id=1, source_target_pairs={{0,20},{4,16},{8,28},{12,24},{16,4},{20,0},{24,12},{28,8},{1,21},{... | collective-permute-start | bytes 405512 | tf_op jit(solution)/shard_map/ppermute | solution.py:877
  80.4 29.0 %collective-permute-start.18 = (bf16[528,128]{1,0:T(8,128)(2,1)}, bf16[528,128]{1,0:T(8,128)(2,1)S(1)}, u32[]{:S(2)}, u32[]{:S(2)}) collective-permute-start(bf16[528,128]{1,0:T(8,128)(2,1)} %get-tuple-element.100), channel_id=1, source_target_pairs={{0,16},{4,20},{8,24},{12,28},{16,0},{20,4},{24,8},{28,12},{1,17},{... | collective-permute-start | bytes 405512 | tf_op jit(solution)/shard_map/ppermute | solution.py:877
  92.1 33.5 %collective-permute-start.20 = (bf16[528,128]{1,0:T(8,128)(2,1)S(1)}, bf16[528,128]{1,0:T(8,128)(2,1)S(1)}, u32[]{:S(2)}, u32[]{:S(2)}) collective-permute-start(bf16[528,128]{1,0:T(8,128)(2,1)S(1)} %copy-done.44), channel_id=1, source_target_pairs={{0,20},{4,16},{8,28},{12,24},{16,4},{20,0},{24,12},{28,8},{1,21},{... | collective-permute-start | bytes 405512 | tf_op jit(solution)/shard_map/ppermute | solution.py:877
  93.3 43.0 %collective-permute-start.15 = (bf16[528,128]{1,0:T(8,128)(2,1)S(1)}, bf16[528,128]{1,0:T(8,128)(2,1)S(1)}, u32[]{:S(2)}, u32[]{:S(2)}) collective-permute-start(bf16[528,128]{1,0:T(8,128)(2,1)S(1)} %copy-done.37), channel_id=1, source_target_pairs={{0,24},{4,28},{8,16},{12,20},{16,8},{20,12},{24,0},{28,4},{1,25},{... | collective-permute-start | bytes 405512 | tf_op jit(solution)/shard_map/ppermute | solution.py:877
  96.0 42.0 %collective-permute-start.17 = (bf16[528,128]{1,0:T(8,128)(2,1)S(1)}, bf16[528,128]{1,0:T(8,128)(2,1)S(1)}, u32[]{:S(2)}, u32[]{:S(2)}) collective-permute-start(bf16[528,128]{1,0:T(8,128)(2,1)S(1)} %copy-done.36), channel_id=1, source_target_pairs={{0,28},{4,24},{8,20},{12,16},{16,12},{20,8},{24,4},{28,0},{1,29},{... | collective-permute-start | bytes 405512 | tf_op jit(solution)/shard_map/ppermute | solution.py:877
  97.3 41.2 %collective-permute-start.16 = (bf16[528,128]{1,0:T(8,128)(2,1)S(1)}, bf16[528,128]{1,0:T(8,128)(2,1)S(1)}, u32[]{:S(2)}, u32[]{:S(2)}) collective-permute-start(bf16[528,128]{1,0:T(8,128)(2,1)S(1)} %copy-done.39), channel_id=1, source_target_pairs={{0,28},{4,24},{8,20},{12,16},{16,12},{20,8},{24,4},{28,0},{1,29},{... | collective-permute-start | bytes 405512 | tf_op jit(solution)/shard_map/ppermute | solution.py:877
  109.4 29.1 %collective-permute-start.7 = (bf16[528,128]{1,0:T(8,128)(2,1)S(1)}, bf16[528,128]{1,0:T(8,128)(2,1)S(1)}, u32[]{:S(2)}, u32[]{:S(2)}) collective-permute-start(bf16[528,128]{1,0:T(8,128)(2,1)S(1)} %copy-done.38), channel_id=1, source_target_pairs={{0,24},{4,28},{8,16},{12,20},{16,8},{20,12},{24,0},{28,4},{1,25},{... | collective-permute-start | bytes 405512 | tf_op jit(solution)/shard_map/ppermute | solution.py:877
  125.6 23.0 %collective-permute-start.28 = (bf16[2,64,128]{2,1,0:T(8,128)(2,1)}, bf16[2,64,128]{2,1,0:T(8,128)(2,1)S(1)}, u32[]{:S(2)}, u32[]{:S(2)}) collective-permute-start(bf16[2,64,128]{2,1,0:T(8,128)(2,1)} %get-tuple-element.132), channel_id=1, source_target_pairs={{0,1},{1,0},{2,3},{3,2},{4,5},{5,4},{6,7},{7,6},{8,9},{9,8},{10,11... | collective-permute-start | bytes 98312 | tf_op jit(solution)/shard_map/ppermute | solution.py:877
  (62 other events, 765.0 us)
where the time goes:
time: 157 us
  starting transfers between devices  73.2 us (47%)
  Pallas kernels  64.6 us (41%)
  waiting for transfers between devices  13.5 us (9%)
  local copies, waits for them, and re-layouts  3.52 us (2%)
    ppermute x34, starting transfers between devices, swap(): return lax.ppermute(value, axis, [(i, i ^ k) for i in range(size)])  73.2 us
    pallas_call x3, Pallas kernels, outputs_part(): pl.pallas_call(functools.partial(outputs_kernel, first, count, bool(earli...  20.7 us
    pallas_call x3, Pallas kernels, states_part(): pl.pallas_call(functools.partial(states_kernel, first, lead), grid_spec=p...  16.4 us
    ppermute x34, waiting for transfers between devices, swap(): return lax.ppermute(value, axis, [(i, i ^ k) for i in range(size)])  13.5 us
    pallas_call x2, Pallas kernels, scores_part(): pl.pallas_call(functools.partial(scores_kernel, count, len(scaled) // 2),...  8.9 us
    pallas_call x2, Pallas kernels, grads_part(): pl.pallas_call(functools.partial(grads_kernel, count, not heads), grid_sp...  8.39 us
    pallas_call x2, Pallas kernels, tree_chunk(): pl.pallas_call(functools.partial(tree_kernel, segs), grid_spec=pltpu.Pref...  7.94 us
  transfers between devices with their start and end apart: 34, of which 8 were waited for; matrix products, arithmetic and copies ran while one was open for 1% of the time, Pallas kernels for 32%

commit v1 on v0

--- a/solution.py
+++ b/solution.py
@@ -519,7 +519,7 @@
     )(place, x, dy, *given, writer, reader)
 
 
-def scores_kernel(count, pairs, _, *refs):
+def scores_kernel(count, pairs, _, __, *refs):
     scaled, (b_ref, c_ref) = refs[: 2 * pairs], refs[2 * pairs : 2 * pairs + 2]
     low_ref, up_ref, gb_ref, gc_ref, acc_ref = refs[2 * pairs + 2 :]
     step = pl.program_id(0)
@@ -547,7 +547,7 @@
         gb_ref[...] = dot(high, c, ((0,), (0,))) + dot(low, c, ((0,), (0,)))
 
 
-def scores_part(first, segs, width, place, scaled, writer, reader):
+def scores_part(first, segs, width, place, scaled, writer, reader, after):
     length, lanes = scaled[0].shape
     count = lanes // width
     _, turn, whole, proj = part_specs(length, width, segs, first)
@@ -557,7 +557,9 @@
         grid_spec=pltpu.PrefetchScalarGridSpec(
             num_scalar_prefetch=1,
             grid=(count,),
-            in_specs=[turn(length)] * len(scaled) + [proj, proj],
+            in_specs=[pl.BlockSpec(memory_space=pl.ANY)]
+            + [turn(length)] * len(scaled)
+            + [proj, proj],
             out_specs=[whole(length, length)] * 2 + [whole(length, N)] * 2,
             scratch_shapes=[pltpu.VMEM((length, length), F32)],
         ),
@@ -565,7 +567,7 @@
         cost_estimate=pl.CostEstimate(
             flops=4 * length * lanes * length, transcendentals=0, bytes_accessed=8 * length * lanes
         ),
-    )(place, *scaled, writer, reader)
+    )(place, after, *scaled, writer, reader)
 
 
 def tree_kernel(segs, place, parents, *refs):
@@ -655,7 +657,17 @@
                 last_ref[:, cols] = tail_row(tail, block)
 
 
-def hand_out(place, outs, accb_ref, accc_ref):
+def grads_shapes(length, heads):
+    if heads:
+        return [jax.ShapeDtypeStruct((2, length // heads, N), BF16)] * heads
+    return [jax.ShapeDtypeStruct((length, N), F32)] * 2
+
+
+def give(place, outs, accb_ref, accc_ref):
+    if outs[0].dtype == F32:
+        outs[0][...] = accb_ref[...]
+        outs[1][...] = accc_ref[...]
+        return
     block = accb_ref.shape[0] // len(outs)
     for k, out in enumerate(outs):
         row = jnp.bitwise_xor(place[0], k) * block
@@ -664,7 +676,7 @@
         out[1] = accc_ref[rows, :].astype(BF16)
 
 
-def grads_kernel(count, whole, place, *refs):
+def grads_kernel(count, place, *refs):
     messages, refs = refs[: count * PIECES], refs[count * PIECES :]
     xs_ref, ys_ref, gb_in, gc_in, *outs, accb_ref, accc_ref, state_ref = refs
     step = pl.program_id(0)
@@ -685,22 +697,16 @@
 
     @pl.when(step == count - 1)
     def _():
-        if whole:
-            outs[0][...] = accb_ref[...]
-            outs[1][...] = accc_ref[...]
-        else:
-            hand_out(place, outs, accb_ref, accc_ref)
+        give(place, outs, accb_ref, accc_ref)
 
 
 def grads_part(first, segs, width, heads, place, messages, xs, ys, gb, gc):
     length, lanes = xs.shape
     count = lanes // width
     _, turn, whole, _ = part_specs(length, width, segs, first)
-    block = jax.ShapeDtypeStruct((2, length // max(heads, 1), N), BF16)
-    total = jax.ShapeDtypeStruct((length, N), F32)
-    outs = [block] * heads if heads else [total, total]
+    outs = grads_shapes(length, heads)
     return pl.pallas_call(
-        functools.partial(grads_kernel, count, not heads),
+        functools.partial(grads_kernel, count),
         grid_spec=pltpu.PrefetchScalarGridSpec(
             num_scalar_prefetch=1,
             grid=(count,),
@@ -719,17 +725,21 @@
     )(place, *messages, xs, ys, gb, gc)
 
 
-def outputs_kernel(first, count, earlier, final, place, *refs):
+def outputs_kernel(first, count, earlier, final, grads, place, *refs):
     messages, refs = refs[: count * PIECES], refs[count * PIECES :]
     x_ref, dy_ref, xs_ref, ys_ref, table_ref, low_ref, up_ref, b_ref, c_ref, skip_ref = refs[:10]
     refs = refs[10:]
     if earlier:
         sums_in, _, _, *refs = refs
     if final:
-        delta_ref, rate_ref, gb_in, gc_in, out_ref, dx_ref, dd_ref, *refs = refs
-        *outs, accb_ref, accc_ref, sums_ref, state_ref, last_ref = refs
-    else:
-        out_ref, dx_ref, sums_ref, state_ref, last_ref = refs
+        delta_ref, rate_ref, *refs = refs
+    if grads:
+        gb_in, gc_in, *refs = refs
+    out_ref, dx_ref, end_ref, *refs = refs
+    *refs, state_ref, last_ref = refs
+    sums_ref = refs.pop() if final else end_ref
+    if grads:
+        *outs, accb_ref, accc_ref = refs
     step = pl.program_id(0)
     length, width = x_ref.shape
     for at in range(count):
@@ -740,7 +750,7 @@
 
     @pl.when(step == 0)
     def _():
-        if final:
+        if grads:
             accb_ref[...] = gb_in[...]
             accc_ref[...] = gc_in[...]
         sums_ref[...] = sums_in[...] if earlier else jnp.zeros_like(sums_ref)
@@ -759,7 +769,7 @@
         skip = skip_ref[:, cols]
         out_ref[:, cols] = (fall * core + skip * x_ref[:, cols].astype(F32)).astype(BF16)
         dx_ref[:, cols] = (grow * grad + skip * dy_ref[:, cols].astype(F32)).astype(BF16)
-        if final:
+        if grads:
             accc_ref[...] += dot(ys, start, NT)
             accb_ref[...] += dot(xs, end, NT)
         direct = xs.astype(F32) * grad
@@ -777,19 +787,25 @@
         high, low = split(at_last, 2)
         sums_ref[length - 8 :, :] += dot(high, pick_through) + dot(low, pick_through)
 
-    if final:
+    if grads:
 
         @pl.when(step == count - 1)
         def _():
-            hand_out(place, outs, accb_ref, accc_ref)
-            both = sums_ref[...].T
+            give(place, outs, accb_ref, accc_ref)
+
+    if final:
+
+        @pl.when(step == count - 1)
+        def _():
+            rate = jnp.concatenate([rate_ref[...], jnp.ones_like(rate_ref)], axis=1)
+            both = (sums_ref[...] * rate).T
             square = (length, length)
             later = onehot(iota(square, 0) >= iota(square, 1))
             back = sum(dot(piece, later) for piece in split(both[:SLOTS], 3))
-            dd_ref[...] = both[SLOTS:] / delta_ref[...] - rate_ref[...] * back
-
-
-def outputs_part(first, segs, place, messages, x, dy, xs, ys, table, low, up, skip, writer, reader, earlier=(), final=(), heads=0):
+            end_ref[...] = both[SLOTS:] / delta_ref[...] - back
+
+
+def outputs_part(first, segs, place, messages, x, dy, xs, ys, table, low, up, skip, writer, reader, earlier=(), final=(), grads=(), heads=0):
     length, lanes = x.shape
     width = lanes // segs
     count = len(messages) // PIECES
@@ -810,23 +826,24 @@
         in_specs += [whole(*sums.shape), any_, any_]
         args += list(earlier)
         aliases = {len(args) - 1: 0, len(args): 1}
-    in_specs += [whole(*value.shape) for value in final]
-    args += list(final)
+    in_specs += [whole(*value.shape) for value in (*final, *grads)]
+    args += [*final, *grads]
     scratch = [pltpu.VMEM((2 * N, width), BF16), pltpu.VMEM((1, width), F32)]
     out_specs, out_shape = [tile(length), tile(length)], [full, full]
+    end = shape(final[0].shape, F32) if final else sums
+    out_specs.append(whole(*end.shape))
+    out_shape.append(end)
     if final:
-        delta = final[0]
-        out_specs.append(whole(*delta.shape))
-        out_shape.append(shape(delta.shape, F32))
-        block = shape((2, length // heads, N), BF16)
-        out_specs += [whole(*block.shape)] * heads
-        out_shape += [block] * heads
-        scratch = [pltpu.VMEM((length, N), F32)] * 2 + [pltpu.VMEM(sums.shape, F32)] + scratch
-    else:
-        out_specs.append(whole(*sums.shape))
-        out_shape.append(sums)
+        scratch = [pltpu.VMEM(sums.shape, F32)] + scratch
+    if grads:
+        scratch = [pltpu.VMEM((length, N), F32)] * 2 + scratch
+        given = grads_shapes(length, heads)
+        out_specs += [whole(*value.shape) for value in given]
+        out_shape += given
     return pl.pallas_call(
-        functools.partial(outputs_kernel, first, count, bool(earlier), bool(final)),
+        functools.partial(
+            outputs_kernel, first, count, bool(earlier), bool(final), bool(grads)
+        ),
         grid_spec=pltpu.PrefetchScalarGridSpec(
             num_scalar_prefetch=1,
             grid=(count,),
@@ -914,25 +931,48 @@
         move(got, own, mid_ks, piece)
         move(got, own, late_ks, piece)
         move(got, own, near_ks, piece)
-    low1, up1, gb1, gc1 = scores_part(mid, segs, width, place, (xs1, ys1, xs2, ys2), b, c)
-    low0, up0, gb0, gc0 = scores_part(0, segs, width, place, (xs0, ys0), b, c)
+    skip = jnp.repeat(skips, P_SIZE)[None, :]
+    scaled = (xs1, ys1, xs2, ys2)
+    low1, up1, gb1, gc1 = scores_part(mid, segs, width, place, scaled, b, c, skip)
+    low0, up0, gb0, gc0 = scores_part(0, segs, width, place, (xs0, ys0), b, c, skip)
     for piece in range(PIECES):
         sent = tree_chunk(segs, place, parents, [got[k, piece] for k in range(segs)])
         sent = {(k, piece): value for k, value in enumerate(sent)}
         move(back, sent, near_ks, piece)
         move(back, sent, mid_ks, piece)
         move(back, sent, late_ks, piece)
-    skip = jnp.repeat(skips, P_SIZE)[None, :]
-    grads0 = grads_part(0, segs, width, heads, place, arrived(near_ks), xs0, ys0, gb0, gc0)
+    common = (table, low0, up0, skip, b, c)
+    out, dx, sums, *grads0 = outputs_part(
+        0,
+        segs,
+        place,
+        arrived(near_ks),
+        x,
+        dy,
+        xs0,
+        ys0,
+        *common,
+        grads=(gb0, gc0),
+        heads=heads,
+    )
     moved0 = [grads0[0]] + [swap(grads0[k], "head", k) for k in range(1, heads)]
-    common = (table, low0, up0, skip, b, c)
-    out, dx, sums = outputs_part(0, segs, place, arrived(near_ks), x, dy, xs0, ys0, *common)
     common = (table, low1, up1, skip, b, c)
-    gb1, gc1 = grads_part(mid, segs, width, 0, place, arrived(mid_ks), xs1, ys1, gb1, gc1)
-    out, dx, sums = outputs_part(
-        mid, segs, place, arrived(mid_ks), x, dy, xs1, ys1, *common, (sums, out, dx)
+    out, dx, sums, gb1, gc1 = outputs_part(
+        mid,
+        segs,
+        place,
+        arrived(mid_ks),
+        x,
+        dy,
+        xs1,
+        ys1,
+        *common,
+        earlier=(sums, out, dx),
+        grads=(gb1, gc1),
     )
-    out, dx, dd, *grads1 = outputs_part(
+    grads1 = grads_part(late, segs, width, heads, place, arrived(late_ks), xs2, ys2, gb1, gc1)
+    moved1 = [grads1[0]] + [swap(grads1[k], "head", k) for k in range(1, heads)]
+    out, dx, dd = outputs_part(
         late,
         segs,
         place,
@@ -942,11 +982,9 @@
         xs2,
         ys2,
         *common,
-        (sums, out, dx),
-        (delta, rates[:, None], gb1, gc1),
-        heads,
+        earlier=(sums, out, dx),
+        final=(delta, rates[None, :]),
     )
-    moved1 = [grads1[0]] + [swap(grads1[k], "head", k) for k in range(1, heads)]
     gb, gc = place_grads(segs, place, moved0, moved1)
     return out[None], dx[None], dd[None], gb[None], gc[None]
 

time: 157 us -> 145 us (0.924)
  starting transfers between devices: 73.2 us -> 50.7 us
  waiting for transfers between devices: 13.5 us -> 27.9 us
  Pallas kernels: 64.6 us -> 60.2 us
    ppermute x34, starting transfers between devices: 73.2 us -> 50.7 us  [swap(): return lax.ppermute(value, axis, [(i, i ^ k) for i in range(size)])]
    ppermute x34, waiting for transfers between devices: 13.5 us -> 27.9 us  [swap(): return lax.ppermute(value, axis, [(i, i ^ k) for i in range(size)])]
    pallas_call x2 -> x1, Pallas kernels: 8.39 us -> 3.38 us  [grads_part(): pl.pallas_call(functools.partial(grads_kernel, count), grid_spec=pltpu.Pr...]
    unnamed x104 -> x92, local copies, waits for them, and re-layouts: 2.05 us -> 3.27 us
  transfers between devices with their start and end apart: 34 -> 34, of which waited for: 8 -> 6; matrix products, arithmetic and copies ran while one was open for 1% -> 1% of each run, Pallas kernels for 32% -> 34%
where the time goes in v1:
time: 145 us
  Pallas kernels  60.2 us (42%)
  starting transfers between devices  50.7 us (35%)
  waiting for transfers between devices  27.9 us (19%)
  local copies, waits for them, and re-layouts  4.03 us (3%)
    ppermute x34, starting transfers between devices, swap(): return lax.ppermute(value, axis, [(i, i ^ k) for i in range(size)])  50.7 us
    ppermute x34, waiting for transfers between devices, swap(): return lax.ppermute(value, axis, [(i, i ^ k) for i in range(size)])  27.9 us
    pallas_call x3, Pallas kernels, outputs_part(): pl.pallas_call(functools.partial(outputs_kernel, first, count, bool(earli...  21.4 us
    pallas_call x3, Pallas kernels, states_part(): pl.pallas_call(functools.partial(states_kernel, first, lead), grid_spec=p...  16.2 us
    pallas_call x2, Pallas kernels, scores_part(): pl.pallas_call(functools.partial(scores_kernel, count, len(scaled) // 2),...  8.87 us
    pallas_call x2, Pallas kernels, tree_chunk(): pl.pallas_call(functools.partial(tree_kernel, segs), grid_spec=pltpu.Pref...  8.04 us
    pallas_call x1, Pallas kernels, grads_part(): pl.pallas_call(functools.partial(grads_kernel, count), grid_spec=pltpu.Pr...  3.38 us
    unnamed x92, local copies, waits for them, and re-layouts  3.27 us
  transfers between devices with their start and end apart: 34, of which 6 were waited for; matrix products, arithmetic and copies ran while one was open for 1% of the time, Pallas kernels for 34%

profile of v1, /device:TPU:0, one launch (start us, length us, event | category | flops | bytes accessed | tf_op | source)
XLA Modules:
  0.0 144.6 jit_solution(844292312907677763)
XLA Ops:
  1.2 4.9 %shard_map.119 = (bf16[528,128]{1,0:T(8,128)(2,1)}, bf16[528,128]{1,0:T(8,128)(2,1)}, bf16[528,128]{1,0:T(8,128)(2,1)}, bf16[528,128]{1,0:T(8,128)(2,1)}, bf16[2...) custom-call(s32[2]{0:T(128)} %pad_add_fusion.place._, bf16[256,4096]{1,0:T(8,128)(2,1)} %bitcast.13, ...), custom_call_target="tpu_custom_call" | custom-call | flops 536870912 | bytes 4194304 | tf_op jit(solution)/shard_map/pallas_call | solution.py:500
  6.1 4.1 %collective-permute-start.3 = (bf16[528,128]{1,0:T(8,128)(2,1)}, bf16[528,128]{1,0:T(8,128)(2,1)S(1)}, u32[]{:S(2)}, u32[]{:S(2)}) collective-permute-start(bf16[528,128]{1,0:T(8,128)(2,1)} %get-tuple-element.78), channel_id=1, source_target_pairs={{0,16},{4,20},{8,24},{12,28},{16,0},{20,4},{24,8},{28,12},{1,17},{... | collective-permute-start | bytes 405512 | tf_op jit(solution)/shard_map/ppermute | solution.py:894
  10.3 2.1 %collective-permute-start.11 = (bf16[528,128]{1,0:T(8,128)(2,1)}, bf16[528,128]{1,0:T(8,128)(2,1)S(1)}, u32[]{:S(2)}, u32[]{:S(2)}) collective-permute-start(bf16[528,128]{1,0:T(8,128)(2,1)} %get-tuple-element.87), channel_id=1, source_target_pairs={{0,16},{4,20},{8,24},{12,28},{16,0},{20,4},{24,8},{28,12},{1,17},{... | collective-permute-start | bytes 405512 | tf_op jit(solution)/shard_map/ppermute | solution.py:894
  12.9 4.5 %shard_map.121 = (bf16[528,128]{1,0:T(8,128)(2,1)}, bf16[528,128]{1,0:T(8,128)(2,1)}, bf16[528,128]{1,0:T(8,128)(2,1)}, bf16[528,128]{1,0:T(8,128)(2,1)}, bf16[2...) custom-call(s32[2]{0:T(128)} %pad_add_fusion.place._, bf16[256,4096]{1,0:T(8,128)(2,1)} %bitcast.14, ...), custom_call_target="tpu_custom_call" | custom-call | flops 536870912 | bytes 4194304 | tf_op jit(solution)/shard_map/pallas_call | solution.py:500
  17.4 3.7 %collective-permute-start.5 = (bf16[528,128]{1,0:T(8,128)(2,1)}, bf16[528,128]{1,0:T(8,128)(2,1)S(1)}, u32[]{:S(2)}, u32[]{:S(2)}) collective-permute-start(bf16[528,128]{1,0:T(8,128)(2,1)} %get-tuple-element.80), channel_id=1, source_target_pairs={{0,24},{4,28},{8,16},{12,20},{16,8},{20,12},{24,0},{28,4},{1,25},{... | collective-permute-start | bytes 405512 | tf_op jit(solution)/shard_map/ppermute | solution.py:894
  21.2 6.8 %shard_map.120 = (bf16[528,128]{1,0:T(8,128)(2,1)}, bf16[528,128]{1,0:T(8,128)(2,1)}, bf16[528,128]{1,0:T(8,128)(2,1)}, bf16[528,128]{1,0:T(8,128)(2,1)}, bf16[5...) custom-call(s32[2]{0:T(128)} %pad_add_fusion.place._, ...), custom_call_target="tpu_custom_call" | custom-call | flops 1073741824 | bytes 8388608 | tf_op jit(solution)/shard_map/pallas_call | solution.py:500
  29.4 2.3 %collective-permute-start.6 = (bf16[528,128]{1,0:T(8,128)(2,1)S(1)}, bf16[528,128]{1,0:T(8,128)(2,1)S(1)}, u32[]{:S(2)}, u32[]{:S(2)}) collective-permute-start(bf16[528,128]{1,0:T(8,128)(2,1)S(1)} %copy-done.42), channel_id=1, source_target_pairs={{0,28},{4,24},{8,20},{12,16},{16,12},{20,8},{24,4},{28,0},{1,29},{... | collective-permute-start | bytes 405512 | tf_op jit(solution)/shard_map/ppermute | solution.py:894
  32.3 5.8 %collective-permute-done.11.refs_4_.refs_12_ = bf16[528,128]{1,0:T(8,128)(2,1)S(1)} collective-permute-done((bf16[528,128]{1,0:T(8,128)(2,1)}, bf16[528,128]{1,0:T(8,128)(2,1)S(1)}, u32[]{:S(2)}, u32[]{:S(2)}) %collective-permute-start.11) | collective-permute-done | bytes 135200 | tf_op jit(solution)/shard_map/ppermute | solution.py:894
  40.6 3.1 %collective-permute-start.13 = (bf16[528,128]{1,0:T(8,128)(2,1)S(1)}, bf16[528,128]{1,0:T(8,128)(2,1)S(1)}, u32[]{:S(2)}, u32[]{:S(2)}) collective-permute-start(bf16[528,128]{1,0:T(8,128)(2,1)S(1)} %copy-done.41), channel_id=1, source_target_pairs={{0,24},{4,28},{8,16},{12,20},{16,8},{20,12},{24,0},{28,4},{1,25},{... | collective-permute-start | bytes 405512 | tf_op jit(solution)/shard_map/ppermute | solution.py:894
  44.7 10.3 %collective-permute-start.9 = (bf16[528,128]{1,0:T(8,128)(2,1)}, bf16[528,128]{1,0:T(8,128)(2,1)S(1)}, u32[]{:S(2)}, u32[]{:S(2)}) collective-permute-start(bf16[528,128]{1,0:T(8,128)(2,1)} %get-tuple-element.85), channel_id=1, source_target_pairs={{0,8},{4,12},{8,0},{12,4},{16,24},{20,28},{24,16},{28,20},{1,9},{5... | collective-permute-start | bytes 405512 | tf_op jit(solution)/shard_map/ppermute | solution.py:894
  55.6 4.1 %tree.2 = (bf16[528,128]{1,0:T(8,128)(2,1)}, bf16[528,128]{1,0:T(8,128)(2,1)}, bf16[528,128]{1,0:T(8,128)(2,1)}, bf16[528,128]{1,0:T(8,128)(2,1)}, bf16[528,128]...) custom-call(s32[2]{0:T(128)} %pad_add_fusion.place._, s32[8]{0:T(128)} %parents.3, ...), custom_call_target="tpu_custom_call" | custom-call | flops 10000000 | bytes 10000000 | tf_op jit(solution)/shard_map/tree/pallas_call | solution.py:628
  64.3 4.0 %tree.3 = (bf16[528,128]{1,0:T(8,128)(2,1)}, bf16[528,128]{1,0:T(8,128)(2,1)}, bf16[528,128]{1,0:T(8,128)(2,1)}, bf16[528,128]{1,0:T(8,128)(2,1)}, bf16[528,128]...) custom-call(s32[2]{0:T(128)} %pad_add_fusion.place._, s32[8]{0:T(128)} %parents.3, ...), custom_call_target="tpu_custom_call" | custom-call | flops 10000000 | bytes 10000000 | tf_op jit(solution)/shard_map/tree/pallas_call | solution.py:628
  68.3 4.9 %collective-permute-done.18.refs_0_ = bf16[528,128]{1,0:T(8,128)(2,1)S(1)} collective-permute-done((bf16[528,128]{1,0:T(8,128)(2,1)}, bf16[528,128]{1,0:T(8,128)(2,1)S(1)}, u32[]{:S(2)}, u32[]{:S(2)}) %collective-permute-start.18) | collective-permute-done | bytes 135200 | tf_op jit(solution)/shard_map/ppermute | solution.py:894
  77.3 3.8 %shard_map.122 = (bf16[256,256]{1,0:T(8,128)(2,1)}, bf16[256,256]{1,0:T(8,128)(2,1)}, f32[256,128]{1,0:T(8,128)}, f32[256,128]{1,0:T(8,128)}) custom-call(s32[2]{0:T(128)} %pad_add_fusion.place._, f32[1,4096]{1,0:T(1,128)} %broadcast_in_dim_reshape.3.__.refs_17_.refs_13_, bf16[256,1024]{1,0:T(8,128)(2,1)} %get-tuple-element.96.refs_0_.refs_6_, ...), custom_call_target="tpu_custom_call" | custom-call | flops 268435456 | bytes 2097152 | tf_op jit(solution)/shard_map/pallas_call | solution.py:555
  81.1 5.0 %shard_map.123 = (bf16[256,256]{1,0:T(8,128)(2,1)}, bf16[256,256]{1,0:T(8,128)(2,1)}, f32[256,128]{1,0:T(8,128)}, f32[256,128]{1,0:T(8,128)}) custom-call(s32[2]{0:T(128)} %pad_add_fusion.place._, f32[1,4096]{1,0:T(1,128)} %broadcast_in_dim_reshape.3.__.refs_17_.refs_13_, bf16[256,2048]{1,0:T(8,128)(2,1)} %get-tuple-element.112.refs_0_.refs_10_, ...), custom_call_target="tpu_custom_call" | custom-call | flops 536870912 | bytes 4194304 | tf_op jit(solution)/shard_map/pallas_call | solution.py:555
  87.6 2.6 %collective-permute-start.16 = (bf16[528,128]{1,0:T(8,128)(2,1)S(1)}, bf16[528,128]{1,0:T(8,128)(2,1)S(1)}, u32[]{:S(2)}, u32[]{:S(2)}) collective-permute-start(bf16[528,128]{1,0:T(8,128)(2,1)S(1)} %copy-done.35), channel_id=1, source_target_pairs={{0,28},{4,24},{8,20},{12,16},{16,12},{20,8},{24,4},{28,0},{1,29},{... | collective-permute-start | bytes 405512 | tf_op jit(solution)/shard_map/ppermute | solution.py:894
  91.4 2.2 %collective-permute-start.17 = (bf16[528,128]{1,0:T(8,128)(2,1)S(1)}, bf16[528,128]{1,0:T(8,128)(2,1)S(1)}, u32[]{:S(2)}, u32[]{:S(2)}) collective-permute-start(bf16[528,128]{1,0:T(8,128)(2,1)S(1)} %copy-done.37), channel_id=1, source_target_pairs={{0,28},{4,24},{8,20},{12,16},{16,12},{20,8},{24,4},{28,0},{1,29},{... | collective-permute-start | bytes 405512 | tf_op jit(solution)/shard_map/ppermute | solution.py:894
  94.2 9.1 %shard_map.124 = (bf16[256,4096]{1,0:T(8,128)(2,1)}, bf16[256,4096]{1,0:T(8,128)(2,1)}, f32[256,128]{1,0:T(8,128)}, bf16[2,64,128]{2,1,0:T(8,128)(2,1)}, bf16[2,...) custom-call(s32[2]{0:T(128)} %pad_add_fusion.place._, ...), custom_call_target="tpu_custom_call" | custom-call | flops 1610612736 | bytes 8388608 | tf_op jit(solution)/shard_map/pallas_call | solution.py:843
  103.4 13.9 %collective-permute-done.21.refs_3_ = bf16[528,128]{1,0:T(8,128)(2,1)S(1)} collective-permute-done((bf16[528,128]{1,0:T(8,128)(2,1)S(1)}, bf16[528,128]{1,0:T(8,128)(2,1)S(1)}, u32[]{:S(2)}, u32[]{:S(2)}) %collective-permute-start.21) | collective-permute-done | bytes 135200 | tf_op jit(solution)/shard_map/ppermute | solution.py:894
  118.0 6.3 %shard_map.125 = (bf16[256,4096]{1,0:T(8,128)(2,1)}, bf16[256,4096]{1,0:T(8,128)(2,1)}, f32[256,128]{1,0:T(8,128)}, f32[256,128]{1,0:T(8,128)}, f32[256,128]{1,0:T(8,128)}) custom-call(s32[2]{0:T(128)} %pad_add_fusion.place._, bf16[528,128]{1,0:T(8,128)(2,1)} %copy-done.18, ...), custom_call_target="tpu_custom_call", output_to_operand_aliasing={{0}: (16, {}), {1}: (17, {})} | custom-call | flops 805306368 | bytes 4194304 | tf_op jit(solution)/shard_map/pallas_call | solution.py:843
  125.1 3.4 %shard_map.127 = (bf16[2,64,128]{2,1,0:T(8,128)(2,1)}, bf16[2,64,128]{2,1,0:T(8,128)(2,1)}, bf16[2,64,128]{2,1,0:T(8,128)(2,1)}, bf16[2,64,128]{2,1,0:T(8,128)(2,1)}) custom-call(s32[2]{0:T(128)} %pad_add_fusion.place._, bf16[528,128]{1,0:T(8,128)(2,1)} %copy-done.14, bf16[528,128]{1,0:T(8,128)(2,1)} %copy-done.16, bf16[528,128]{1,0:T(8,128)(2,1)} %copy-done.15, ...), custom_call_target="tpu_custom_call" | custom-call | flops 134217728 | bytes 2097152 | tf_op jit(solution)/shard_map/pallas_call | solution.py:708
  128.5 1.5 %collective-permute-start.31 = (bf16[2,64,128]{2,1,0:T(8,128)(2,1)}, bf16[2,64,128]{2,1,0:T(8,128)(2,1)S(1)}, u32[]{:S(2)}, u32[]{:S(2)}) collective-permute-start(bf16[2,64,128]{2,1,0:T(8,128)(2,1)} %get-tuple-element.136), channel_id=1, source_target_pairs={{0,1},{1,0},{2,3},{3,2},{4,5},{5,4},{6,7},{7,6},{8,9},{9,8},{10,11... | collective-permute-start | bytes 98312 | tf_op jit(solution)/shard_map/ppermute | solution.py:894
  135.6 6.0 %shard_map.126 = (bf16[256,4096]{1,0:T(8,128)(2,1)}, bf16[256,4096]{1,0:T(8,128)(2,1)}, f32[64,256]{1,0:T(8,128)}) custom-call(s32[2]{0:T(128)} %pad_add_fusion.place._, bf16[528,128]{1,0:T(8,128)(2,1)} %copy-done.14, bf16[528,128]{1,0:T(8,128)(2,1)} %copy-done.16, bf16[528,128]{1,0:T(8,128)(2,1)} %copy-done.15, ...), custom_call_target="tpu_custom_call", output_to_operand_aliasing={{0}: (16, {}), {1}: (17, {})} | custom-call | flops 805306368 | bytes 4194304 | tf_op jit(solution)/shard_map/pallas_call | solution.py:843
  142.3 2.3 %place_grads.1 = (bf16[64,1024]{1,0:T(8,128)(2,1)}, bf16[64,1024]{1,0:T(8,128)(2,1)}) custom-call(s32[2]{0:T(128)} %pad_add_fusion.place._, bf16[2,64,128]{2,1,0:T(8,128)(2,1)} %get-tuple-element.129.refs_0_, bf16[2,64,128]{2,1,0:T(8,128)(2,1)} %copy-done.31, bf16[2,64,128]{2,1,0:T(8,128)(2,1)} %copy-done.32, bf16[2,64,128]{2,1,0:T(8,128)(2,1)} %copy-done.33, ...), custom_call_target="tpu_custom_call" | custom-call | tf_op jit(solution)/shard_map/place_grads/pallas_call | solution.py:879
  (151 shorter events, 26.7 us)
Async XLA Ops:
  6.1 23.3 %collective-permute-start.3 = (bf16[528,128]{1,0:T(8,128)(2,1)}, bf16[528,128]{1,0:T(8,128)(2,1)S(1)}, u32[]{:S(2)}, u32[]{:S(2)}) collective-permute-start(bf16[528,128]{1,0:T(8,128)(2,1)} %get-tuple-element.78), channel_id=1, source_target_pairs={{0,16},{4,20},{8,24},{12,28},{16,0},{20,4},{24,8},{28,12},{1,17},{... | collective-permute-start | bytes 405512 | tf_op jit(solution)/shard_map/ppermute | solution.py:894
  10.3 21.4 %collective-permute-start.4 = (bf16[528,128]{1,0:T(8,128)(2,1)}, bf16[528,128]{1,0:T(8,128)(2,1)S(1)}, u32[]{:S(2)}, u32[]{:S(2)}) collective-permute-start(bf16[528,128]{1,0:T(8,128)(2,1)} %get-tuple-element.79), channel_id=1, source_target_pairs={{0,20},{4,16},{8,28},{12,24},{16,4},{20,0},{24,12},{28,8},{1,21},{... | collective-permute-start | bytes 405512 | tf_op jit(solution)/shard_map/ppermute | solution.py:894
  10.3 27.8 %collective-permute-start.11 = (bf16[528,128]{1,0:T(8,128)(2,1)}, bf16[528,128]{1,0:T(8,128)(2,1)S(1)}, u32[]{:S(2)}, u32[]{:S(2)}) collective-permute-start(bf16[528,128]{1,0:T(8,128)(2,1)} %get-tuple-element.87), channel_id=1, source_target_pairs={{0,16},{4,20},{8,24},{12,28},{16,0},{20,4},{24,8},{28,12},{1,17},{... | collective-permute-start | bytes 405512 | tf_op jit(solution)/shard_map/ppermute | solution.py:894
  12.3 26.9 %collective-permute-start.12 = (bf16[528,128]{1,0:T(8,128)(2,1)}, bf16[528,128]{1,0:T(8,128)(2,1)S(1)}, u32[]{:S(2)}, u32[]{:S(2)}) collective-permute-start(bf16[528,128]{1,0:T(8,128)(2,1)} %get-tuple-element.88), channel_id=1, source_target_pairs={{0,20},{4,16},{8,28},{12,24},{16,4},{20,0},{24,12},{28,8},{1,21},{... | collective-permute-start | bytes 405512 | tf_op jit(solution)/shard_map/ppermute | solution.py:894
  17.4 23.1 %collective-permute-start.5 = (bf16[528,128]{1,0:T(8,128)(2,1)}, bf16[528,128]{1,0:T(8,128)(2,1)S(1)}, u32[]{:S(2)}, u32[]{:S(2)}) collective-permute-start(bf16[528,128]{1,0:T(8,128)(2,1)} %get-tuple-element.80), channel_id=1, source_target_pairs={{0,24},{4,28},{8,16},{12,20},{16,8},{20,12},{24,0},{28,4},{1,25},{... | collective-permute-start | bytes 405512 | tf_op jit(solution)/shard_map/ppermute | solution.py:894
  29.4 14.3 %collective-permute-start.6 = (bf16[528,128]{1,0:T(8,128)(2,1)S(1)}, bf16[528,128]{1,0:T(8,128)(2,1)S(1)}, u32[]{:S(2)}, u32[]{:S(2)}) collective-permute-start(bf16[528,128]{1,0:T(8,128)(2,1)S(1)} %copy-done.42), channel_id=1, source_target_pairs={{0,28},{4,24},{8,20},{12,16},{16,12},{20,8},{24,4},{28,0},{1,29},{... | collective-permute-start | bytes 405512 | tf_op jit(solution)/shard_map/ppermute | solution.py:894
  39.3 15.7 %collective-permute-start.2 = (bf16[528,128]{1,0:T(8,128)(2,1)}, bf16[528,128]{1,0:T(8,128)(2,1)S(1)}, u32[]{:S(2)}, u32[]{:S(2)}) collective-permute-start(bf16[528,128]{1,0:T(8,128)(2,1)} %get-tuple-element.77), channel_id=1, source_target_pairs={{0,12},{4,8},{8,4},{12,0},{16,28},{20,24},{24,20},{28,16},{1,13},{... | collective-permute-start | bytes 405512 | tf_op jit(solution)/shard_map/ppermute | solution.py:894
  40.6 19.1 %collective-permute-start.13 = (bf16[528,128]{1,0:T(8,128)(2,1)S(1)}, bf16[528,128]{1,0:T(8,128)(2,1)S(1)}, u32[]{:S(2)}, u32[]{:S(2)}) collective-permute-start(bf16[528,128]{1,0:T(8,128)(2,1)S(1)} %copy-done.41), channel_id=1, source_target_pairs={{0,24},{4,28},{8,16},{12,20},{16,8},{20,12},{24,0},{28,4},{1,25},{... | collective-permute-start | bytes 405512 | tf_op jit(solution)/shard_map/ppermute | solution.py:894
  43.7 16.7 %collective-permute-start.14 = (bf16[528,128]{1,0:T(8,128)(2,1)S(1)}, bf16[528,128]{1,0:T(8,128)(2,1)S(1)}, u32[]{:S(2)}, u32[]{:S(2)}) collective-permute-start(bf16[528,128]{1,0:T(8,128)(2,1)S(1)} %copy-done.40), channel_id=1, source_target_pairs={{0,28},{4,24},{8,20},{12,16},{16,12},{20,8},{24,4},{28,0},{1,29},{... | collective-permute-start | bytes 405512 | tf_op jit(solution)/shard_map/ppermute | solution.py:894
  44.4 17.4 %collective-permute-start.8 = (bf16[528,128]{1,0:T(8,128)(2,1)}, bf16[528,128]{1,0:T(8,128)(2,1)S(1)}, u32[]{:S(2)}, u32[]{:S(2)}) collective-permute-start(bf16[528,128]{1,0:T(8,128)(2,1)} %get-tuple-element.84), channel_id=1, source_target_pairs={{0,4},{4,0},{8,12},{12,8},{16,20},{20,16},{24,28},{28,24},{1,5},{5... | collective-permute-start | bytes 405512 | tf_op jit(solution)/shard_map/ppermute | solution.py:894
  44.7 18.2 %collective-permute-start.9 = (bf16[528,128]{1,0:T(8,128)(2,1)}, bf16[528,128]{1,0:T(8,128)(2,1)S(1)}, u32[]{:S(2)}, u32[]{:S(2)}) collective-permute-start(bf16[528,128]{1,0:T(8,128)(2,1)} %get-tuple-element.85), channel_id=1, source_target_pairs={{0,8},{4,12},{8,0},{12,4},{16,24},{20,28},{24,16},{28,20},{1,9},{5... | collective-permute-start | bytes 405512 | tf_op jit(solution)/shard_map/ppermute | solution.py:894
  59.7 13.5 %collective-permute-start.18 = (bf16[528,128]{1,0:T(8,128)(2,1)}, bf16[528,128]{1,0:T(8,128)(2,1)S(1)}, u32[]{:S(2)}, u32[]{:S(2)}) collective-permute-start(bf16[528,128]{1,0:T(8,128)(2,1)} %get-tuple-element.100), channel_id=1, source_target_pairs={{0,16},{4,20},{8,24},{12,28},{16,0},{20,4},{24,8},{28,12},{1,17},{... | collective-permute-start | bytes 405512 | tf_op jit(solution)/shard_map/ppermute | solution.py:894
  60.3 13.5 %collective-permute-start.20 = (bf16[528,128]{1,0:T(8,128)(2,1)}, bf16[528,128]{1,0:T(8,128)(2,1)S(1)}, u32[]{:S(2)}, u32[]{:S(2)}) collective-permute-start(bf16[528,128]{1,0:T(8,128)(2,1)} %get-tuple-element.102), channel_id=1, source_target_pairs={{0,20},{4,16},{8,28},{12,24},{16,4},{20,0},{24,12},{28,8},{1,21},{... | collective-permute-start | bytes 405512 | tf_op jit(solution)/shard_map/ppermute | solution.py:894
  61.9 13.2 %collective-permute-start.22 = (bf16[528,128]{1,0:T(8,128)(2,1)}, bf16[528,128]{1,0:T(8,128)(2,1)S(1)}, u32[]{:S(2)}, u32[]{:S(2)}) collective-permute-start(bf16[528,128]{1,0:T(8,128)(2,1)} %get-tuple-element.106), channel_id=1, source_target_pairs={{0,4},{4,0},{8,12},{12,8},{16,20},{20,16},{24,28},{28,24},{1,5},{5... | collective-permute-start | bytes 405512 | tf_op jit(solution)/shard_map/ppermute | solution.py:894
  63.6 22.6 %collective-permute-start.26 = (bf16[528,128]{1,0:T(8,128)(2,1)}, bf16[528,128]{1,0:T(8,128)(2,1)S(1)}, u32[]{:S(2)}, u32[]{:S(2)}) collective-permute-start(bf16[528,128]{1,0:T(8,128)(2,1)} %get-tuple-element.110), channel_id=1, source_target_pairs={{0,12},{4,8},{8,4},{12,0},{16,28},{20,24},{24,20},{28,16},{1,13},{... | collective-permute-start | bytes 405512 | tf_op jit(solution)/shard_map/ppermute | solution.py:894
  73.2 14.4 %collective-permute-start.19 = (bf16[528,128]{1,0:T(8,128)(2,1)}, bf16[528,128]{1,0:T(8,128)(2,1)S(1)}, u32[]{:S(2)}, u32[]{:S(2)}) collective-permute-start(bf16[528,128]{1,0:T(8,128)(2,1)} %get-tuple-element.101), channel_id=1, source_target_pairs={{0,16},{4,20},{8,24},{12,28},{16,0},{20,4},{24,8},{28,12},{1,17},{... | collective-permute-start | bytes 405512 | tf_op jit(solution)/shard_map/ppermute | solution.py:894
  73.9 16.4 %collective-permute-start.23 = (bf16[528,128]{1,0:T(8,128)(2,1)}, bf16[528,128]{1,0:T(8,128)(2,1)S(1)}, u32[]{:S(2)}, u32[]{:S(2)}) collective-permute-start(bf16[528,128]{1,0:T(8,128)(2,1)} %get-tuple-element.107), channel_id=1, source_target_pairs={{0,4},{4,0},{8,12},{12,8},{16,20},{20,16},{24,28},{28,24},{1,5},{5... | collective-permute-start | bytes 405512 | tf_op jit(solution)/shard_map/ppermute | solution.py:894
  75.1 16.3 %collective-permute-start.25 = (bf16[528,128]{1,0:T(8,128)(2,1)}, bf16[528,128]{1,0:T(8,128)(2,1)S(1)}, u32[]{:S(2)}, u32[]{:S(2)}) collective-permute-start(bf16[528,128]{1,0:T(8,128)(2,1)} %get-tuple-element.109), channel_id=1, source_target_pairs={{0,8},{4,12},{8,0},{12,4},{16,24},{20,28},{24,16},{28,20},{1,9},{5... | collective-permute-start | bytes 405512 | tf_op jit(solution)/shard_map/ppermute | solution.py:894
  75.1 18.5 %collective-permute-start.27 = (bf16[528,128]{1,0:T(8,128)(2,1)}, bf16[528,128]{1,0:T(8,128)(2,1)S(1)}, u32[]{:S(2)}, u32[]{:S(2)}) collective-permute-start(bf16[528,128]{1,0:T(8,128)(2,1)} %get-tuple-element.111), channel_id=1, source_target_pairs={{0,12},{4,8},{8,4},{12,0},{16,28},{20,24},{24,20},{28,16},{1,13},{... | collective-permute-start | bytes 405512 | tf_op jit(solution)/shard_map/ppermute | solution.py:894
  86.2 38.0 %collective-permute-start.7 = (bf16[528,128]{1,0:T(8,128)(2,1)S(1)}, bf16[528,128]{1,0:T(8,128)(2,1)S(1)}, u32[]{:S(2)}, u32[]{:S(2)}) collective-permute-start(bf16[528,128]{1,0:T(8,128)(2,1)S(1)} %copy-done.36), channel_id=1, source_target_pairs={{0,24},{4,28},{8,16},{12,20},{16,8},{20,12},{24,0},{28,4},{1,25},{... | collective-permute-start | bytes 405512 | tf_op jit(solution)/shard_map/ppermute | solution.py:894
  87.6 36.7 %collective-permute-start.16 = (bf16[528,128]{1,0:T(8,128)(2,1)S(1)}, bf16[528,128]{1,0:T(8,128)(2,1)S(1)}, u32[]{:S(2)}, u32[]{:S(2)}) collective-permute-start(bf16[528,128]{1,0:T(8,128)(2,1)S(1)} %copy-done.35), channel_id=1, source_target_pairs={{0,28},{4,24},{8,20},{12,16},{16,12},{20,8},{24,4},{28,0},{1,29},{... | collective-permute-start | bytes 405512 | tf_op jit(solution)/shard_map/ppermute | solution.py:894
  90.2 34.1 %collective-permute-start.15 = (bf16[528,128]{1,0:T(8,128)(2,1)S(1)}, bf16[528,128]{1,0:T(8,128)(2,1)S(1)}, u32[]{:S(2)}, u32[]{:S(2)}) collective-permute-start(bf16[528,128]{1,0:T(8,128)(2,1)S(1)} %copy-done.38), channel_id=1, source_target_pairs={{0,24},{4,28},{8,16},{12,20},{16,8},{20,12},{24,0},{28,4},{1,25},{... | collective-permute-start | bytes 405512 | tf_op jit(solution)/shard_map/ppermute | solution.py:894
  91.4 32.9 %collective-permute-start.17 = (bf16[528,128]{1,0:T(8,128)(2,1)S(1)}, bf16[528,128]{1,0:T(8,128)(2,1)S(1)}, u32[]{:S(2)}, u32[]{:S(2)}) collective-permute-start(bf16[528,128]{1,0:T(8,128)(2,1)S(1)} %copy-done.37), channel_id=1, source_target_pairs={{0,28},{4,24},{8,20},{12,16},{16,12},{20,8},{24,4},{28,0},{1,29},{... | collective-permute-start | bytes 405512 | tf_op jit(solution)/shard_map/ppermute | solution.py:894
  93.6 23.7 %collective-permute-start.21 = (bf16[528,128]{1,0:T(8,128)(2,1)S(1)}, bf16[528,128]{1,0:T(8,128)(2,1)S(1)}, u32[]{:S(2)}, u32[]{:S(2)}) collective-permute-start(bf16[528,128]{1,0:T(8,128)(2,1)S(1)} %copy-done.39), channel_id=1, source_target_pairs={{0,20},{4,16},{8,28},{12,24},{16,4},{20,0},{24,12},{28,8},{1,21},{... | collective-permute-start | bytes 405512 | tf_op jit(solution)/shard_map/ppermute | solution.py:894
  (56 other events, 516.0 us)

commit v2 on v1

--- a/solution.py
+++ b/solution.py
@@ -478,9 +478,12 @@
             message[message.shape[0] - EXTRA :, :] = tail.astype(BF16)
 
 
-def part_specs(length, width, segs, first):
-    tile = lambda rows: pl.BlockSpec((rows, width), lambda i, f: (0, chunk_of(f, first + i)))
-    turn = lambda rows: pl.BlockSpec((rows, width), lambda i, f: (0, i))
+def part_specs(length, width, segs, first, pieces=1, piece=0):
+    part = width // pieces
+    tile = lambda rows: pl.BlockSpec(
+        (rows, part), lambda i, f: (0, chunk_of(f, first + i) * pieces + piece)
+    )
+    turn = lambda rows: pl.BlockSpec((rows, part), lambda i, f: (0, i * pieces + piece))
     whole = lambda *shape: pl.BlockSpec(shape, lambda i, f: (0,) * len(shape))
     proj = pl.BlockSpec(
         (length, N), lambda i, f: (0, 2 * f[0] + group_of(chunk_of(f, first), segs))
@@ -646,11 +649,11 @@
 
 
 def unpack(messages, state_ref, last_ref):
-    blocks = state_ref.shape[1] // LANES // PIECES
-    for piece, message in enumerate(messages):
+    blocks = state_ref.shape[1] // LANES // len(messages)
+    for at, message in enumerate(messages):
         tail = message[2 * N * blocks :, :]
         for block in range(blocks):
-            lane = (piece * blocks + block) * LANES
+            lane = (at * blocks + block) * LANES
             cols = slice(lane, lane + LANES)
             state_ref[:, cols] = message[2 * N * block : 2 * N * (block + 1), :]
             if last_ref is not None:
@@ -677,7 +680,7 @@
 
 
 def grads_kernel(count, place, *refs):
-    messages, refs = refs[: count * PIECES], refs[count * PIECES :]
+    messages, refs = refs[:count], refs[count:]
     xs_ref, ys_ref, gb_in, gc_in, *outs, accb_ref, accc_ref, state_ref = refs
     step = pl.program_id(0)
 
@@ -689,8 +692,8 @@
     for at in range(count):
 
         @pl.when(step == at)
-        def _(parts=messages[at * PIECES : (at + 1) * PIECES]):
-            unpack(parts, state_ref, None)
+        def _(message=messages[at]):
+            unpack([message], state_ref, None)
 
     accc_ref[...] += dot(ys_ref[...], state_ref[:N, :], NT)
     accb_ref[...] += dot(xs_ref[...], state_ref[N:, :], NT)
@@ -700,10 +703,10 @@
         give(place, outs, accb_ref, accc_ref)
 
 
-def grads_part(first, segs, width, heads, place, messages, xs, ys, gb, gc):
+def grads_part(first, piece, segs, width, heads, place, messages, xs, ys, gb, gc):
     length, lanes = xs.shape
     count = lanes // width
-    _, turn, whole, _ = part_specs(length, width, segs, first)
+    _, turn, whole, _ = part_specs(length, width, segs, first, PIECES, piece)
     outs = grads_shapes(length, heads)
     return pl.pallas_call(
         functools.partial(grads_kernel, count),
@@ -714,7 +717,7 @@
             + [turn(length)] * 2
             + [whole(length, N)] * 2,
             out_specs=[whole(*out.shape) for out in outs],
-            scratch_shapes=[pltpu.VMEM((length, N), F32)] * 2 + [pltpu.VMEM((2 * N, width), BF16)],
+            scratch_shapes=[pltpu.VMEM((length, N), F32)] * 2 + [pltpu.VMEM((2 * N, width // PIECES), BF16)],
         ),
         out_shape=outs,
         cost_estimate=pl.CostEstimate(
@@ -725,8 +728,8 @@
     )(place, *messages, xs, ys, gb, gc)
 
 
-def outputs_kernel(first, count, earlier, final, grads, place, *refs):
-    messages, refs = refs[: count * PIECES], refs[count * PIECES :]
+def outputs_kernel(first, piece, per, count, earlier, final, grads, place, *refs):
+    messages, refs = refs[: count * per], refs[count * per :]
     x_ref, dy_ref, xs_ref, ys_ref, table_ref, low_ref, up_ref, b_ref, c_ref, skip_ref = refs[:10]
     refs = refs[10:]
     if earlier:
@@ -745,7 +748,7 @@
     for at in range(count):
 
         @pl.when(step == at)
-        def _(parts=messages[at * PIECES : (at + 1) * PIECES]):
+        def _(parts=messages[at * per : (at + 1) * per]):
             unpack(parts, state_ref, last_ref)
 
     @pl.when(step == 0)
@@ -758,7 +761,7 @@
     chunk = chunk_of(place, step + first)
     for at in range(0, width, TILE):
         cols = slice(at, at + TILE)
-        lane = chunk * width + at
+        lane = (chunk * (PIECES // per) + piece) * width + at
         lanes = spread_at(lane)
         fall = dot(table_ref[0], lanes)
         grow = dot(table_ref[1], lanes)
@@ -805,11 +808,13 @@
             end_ref[...] = both[SLOTS:] / delta_ref[...] - back
 
 
-def outputs_part(first, segs, place, messages, x, dy, xs, ys, table, low, up, skip, writer, reader, earlier=(), final=(), grads=(), heads=0):
+def outputs_part(first, piece, per, segs, place, messages, x, dy, xs, ys, table, low, up, skip, writer, reader, earlier=(), final=(), grads=(), heads=0):
     length, lanes = x.shape
     width = lanes // segs
-    count = len(messages) // PIECES
-    tile, turn, whole, proj = part_specs(length, width, segs, first)
+    count = len(messages) // per
+    tile, turn, whole, proj = part_specs(
+        length, width, segs, first, PIECES // per, piece
+    )
     shape = jax.ShapeDtypeStruct
     sums = shape((length, 2 * SLOTS), F32)
     full = shape((length, lanes), BF16)
@@ -828,7 +833,8 @@
         aliases = {len(args) - 1: 0, len(args): 1}
     in_specs += [whole(*value.shape) for value in (*final, *grads)]
     args += [*final, *grads]
-    scratch = [pltpu.VMEM((2 * N, width), BF16), pltpu.VMEM((1, width), F32)]
+    part = width * per // PIECES
+    scratch = [pltpu.VMEM((2 * N, part), BF16), pltpu.VMEM((1, part), F32)]
     out_specs, out_shape = [tile(length), tile(length)], [full, full]
     end = shape(final[0].shape, F32) if final else sums
     out_specs.append(whole(*end.shape))
@@ -842,7 +848,7 @@
         out_shape += given
     return pl.pallas_call(
         functools.partial(
-            outputs_kernel, first, count, bool(earlier), bool(final), bool(grads)
+            outputs_kernel, first, piece, per, count, bool(earlier), bool(final), bool(grads)
         ),
         grid_spec=pltpu.PrefetchScalarGridSpec(
             num_scalar_prefetch=1,
@@ -913,8 +919,8 @@
         for k in ks:
             out[k, piece] = swap(values[k, piece], "seg", k) if k else values[k, piece]
 
-    def arrived(ks):
-        return [back[k, piece] for k in ks for piece in range(PIECES)]
+    def arrived(ks, pieces):
+        return [back[k, piece] for k in ks for piece in pieces]
 
     *parts, xs1, ys1, table = states_part(
         mid, late - mid, segs, place, x, dy, (delta, rates[None, :]), b, c
@@ -941,50 +947,48 @@
         move(back, sent, near_ks, piece)
         move(back, sent, mid_ks, piece)
         move(back, sent, late_ks, piece)
-    common = (table, low0, up0, skip, b, c)
-    out, dx, sums, *grads0 = outputs_part(
-        0,
-        segs,
-        place,
-        arrived(near_ks),
-        x,
-        dy,
-        xs0,
-        ys0,
-        *common,
-        grads=(gb0, gc0),
-        heads=heads,
+    near = (0, near_ks, xs0, ys0, low0, up0)
+    middle = (mid, mid_ks, xs1, ys1, low1, up1)
+    last = (late, late_ks, xs2, ys2, low1, up1)
+    so_far = ()
+
+    def outputs(chunks, pieces, **more):
+        nonlocal so_far
+        first, ks, xs, ys, low, up = chunks
+        out, dx, sums, *grads = outputs_part(
+            first,
+            pieces[0],
+            len(pieces),
+            segs,
+            place,
+            arrived(ks, pieces),
+            x,
+            dy,
+            xs,
+            ys,
+            table,
+            low,
+            up,
+            skip,
+            b,
+            c,
+            earlier=so_far,
+            **more,
+        )
+        so_far = (sums, out, dx)
+        return grads
+
+    both = range(PIECES)
+    grads0 = outputs(near, both, grads=(gb0, gc0), heads=heads)
+    moved0 = [grads0[0]] + [swap(grads0[k], "head", k) for k in range(1, heads)]
+    gb1, gc1 = outputs(last, (0,), grads=(gb1, gc1))
+    gb1, gc1 = outputs(middle, both, grads=(gb1, gc1))
+    grads1 = grads_part(
+        late, 1, segs, width, heads, place, arrived(late_ks, (1,)), xs2, ys2, gb1, gc1
     )
-    moved0 = [grads0[0]] + [swap(grads0[k], "head", k) for k in range(1, heads)]
-    common = (table, low1, up1, skip, b, c)
-    out, dx, sums, gb1, gc1 = outputs_part(
-        mid,
-        segs,
-        place,
-        arrived(mid_ks),
-        x,
-        dy,
-        xs1,
-        ys1,
-        *common,
-        earlier=(sums, out, dx),
-        grads=(gb1, gc1),
-    )
-    grads1 = grads_part(late, segs, width, heads, place, arrived(late_ks), xs2, ys2, gb1, gc1)
     moved1 = [grads1[0]] + [swap(grads1[k], "head", k) for k in range(1, heads)]
-    out, dx, dd = outputs_part(
-        late,
-        segs,
-        place,
-        arrived(late_ks),
-        x,
-        dy,
-        xs2,
-        ys2,
-        *common,
-        earlier=(sums, out, dx),
-        final=(delta, rates[None, :]),
-    )
+    outputs(last, (1,), final=(delta, rates[None, :]))
+    dd, out, dx = so_far
     gb, gc = place_grads(segs, place, moved0, moved1)
     return out[None], dx[None], dd[None], gb[None], gc[None]
 

time: 145 us -> 146 us (level)
  the two profiles are of different devices: /device:TPU:0 before, /device:TPU:14 now
where the time goes in v2:
time: 146 us; the launch traced here: 145 us
  Pallas kernels  63.5 us (43%)
  starting transfers between devices  43.7 us (30%)
  waiting for transfers between devices  32.6 us (22%)
  local copies, waits for them, and re-layouts  3.51 us (2%)
    ppermute x34, starting transfers between devices, swap(): return lax.ppermute(value, axis, [(i, i ^ k) for i in range(size)])  43.7 us
    ppermute x34, waiting for transfers between devices, swap(): return lax.ppermute(value, axis, [(i, i ^ k) for i in range(size)])  32.6 us
    pallas_call x4, Pallas kernels, outputs_part(): pl.pallas_call(functools.partial(outputs_kernel, first, piece, per, count...  24.9 us
    pallas_call x3, Pallas kernels, states_part(): pl.pallas_call(functools.partial(states_kernel, first, lead), grid_spec=p...  16.4 us
    pallas_call x2, Pallas kernels, scores_part(): pl.pallas_call(functools.partial(scores_kernel, count, len(scaled) // 2),...  8.87 us
    pallas_call x2, Pallas kernels, tree_chunk(): pl.pallas_call(functools.partial(tree_kernel, segs), grid_spec=pltpu.Pref...  7.87 us
    pallas_call x1, Pallas kernels, grads_part(): pl.pallas_call(functools.partial(grads_kernel, count), grid_spec=pltpu.Pr...  3.11 us
  transfers between devices with their start and end apart: 34, of which 7 were waited for; matrix products, arithmetic and copies ran while one was open for 1% of the time, Pallas kernels for 37%

profile of v2, /device:TPU:14, one launch (start us, length us, event | category | flops | bytes accessed | tf_op | source)
XLA Modules:
  0.0 145.0 jit_solution(6184546385014257781)
XLA Ops:
  1.2 4.9 %shard_map.119 = (bf16[528,128]{1,0:T(8,128)(2,1)}, bf16[528,128]{1,0:T(8,128)(2,1)}, bf16[528,128]{1,0:T(8,128)(2,1)}, bf16[528,128]{1,0:T(8,128)(2,1)}, bf16[2...) custom-call(s32[2]{0:T(128)} %pad_add_fusion.place._, bf16[256,4096]{1,0:T(8,128)(2,1)} %bitcast.13, ...), custom_call_target="tpu_custom_call" | custom-call | flops 536870912 | bytes 4194304 | tf_op jit(solution)/shard_map/pallas_call | solution.py:503
  6.1 2.7 %collective-permute-start.3 = (bf16[528,128]{1,0:T(8,128)(2,1)}, bf16[528,128]{1,0:T(8,128)(2,1)S(1)}, u32[]{:S(2)}, u32[]{:S(2)}) collective-permute-start(bf16[528,128]{1,0:T(8,128)(2,1)} %get-tuple-element.83), channel_id=1, source_target_pairs={{0,16},{4,20},{8,24},{12,28},{16,0},{20,4},{24,8},{28,12},{1,17},{... | collective-permute-start | bytes 405512 | tf_op jit(solution)/shard_map/ppermute | solution.py:900
  8.8 2.1 %collective-permute-start.12 = (bf16[528,128]{1,0:T(8,128)(2,1)}, bf16[528,128]{1,0:T(8,128)(2,1)S(1)}, u32[]{:S(2)}, u32[]{:S(2)}) collective-permute-start(bf16[528,128]{1,0:T(8,128)(2,1)} %get-tuple-element.99), channel_id=1, source_target_pairs={{0,16},{4,20},{8,24},{12,28},{16,0},{20,4},{24,8},{28,12},{1,17},{... | collective-permute-start | bytes 405512 | tf_op jit(solution)/shard_map/ppermute | solution.py:900
  11.5 4.6 %shard_map.121 = (bf16[528,128]{1,0:T(8,128)(2,1)}, bf16[528,128]{1,0:T(8,128)(2,1)}, bf16[528,128]{1,0:T(8,128)(2,1)}, bf16[528,128]{1,0:T(8,128)(2,1)}, bf16[2...) custom-call(s32[2]{0:T(128)} %pad_add_fusion.place._, bf16[256,4096]{1,0:T(8,128)(2,1)} %bitcast.14, ...), custom_call_target="tpu_custom_call" | custom-call | flops 536870912 | bytes 4194304 | tf_op jit(solution)/shard_map/pallas_call | solution.py:503
  17.6 8.8 %collective-permute-done.3.refs_4_.refs_12_ = bf16[528,128]{1,0:T(8,128)(2,1)S(1)} collective-permute-done((bf16[528,128]{1,0:T(8,128)(2,1)}, bf16[528,128]{1,0:T(8,128)(2,1)S(1)}, u32[]{:S(2)}, u32[]{:S(2)}) %collective-permute-start.3) | collective-permute-done | bytes 135200 | tf_op jit(solution)/shard_map/ppermute | solution.py:900
  26.4 6.9 %shard_map.120 = (bf16[528,128]{1,0:T(8,128)(2,1)}, bf16[528,128]{1,0:T(8,128)(2,1)}, bf16[528,128]{1,0:T(8,128)(2,1)}, bf16[528,128]{1,0:T(8,128)(2,1)}, bf16[5...) custom-call(s32[2]{0:T(128)} %pad_add_fusion.place._, ...), custom_call_target="tpu_custom_call" | custom-call | flops 1073741824 | bytes 8388608 | tf_op jit(solution)/shard_map/pallas_call | solution.py:503
  35.0 3.1 %collective-permute-start.1 = (bf16[528,128]{1,0:T(8,128)(2,1)}, bf16[528,128]{1,0:T(8,128)(2,1)S(1)}, u32[]{:S(2)}, u32[]{:S(2)}) collective-permute-start(bf16[528,128]{1,0:T(8,128)(2,1)} %get-tuple-element.81), channel_id=1, source_target_pairs={{0,8},{4,12},{8,0},{12,4},{16,24},{20,28},{24,16},{28,20},{1,9},{5... | collective-permute-start | bytes 405512 | tf_op jit(solution)/shard_map/ppermute | solution.py:900
  39.7 2.0 %collective-permute-done.5.refs_6_.refs_14_ = bf16[528,128]{1,0:T(8,128)(2,1)S(1)} collective-permute-done((bf16[528,128]{1,0:T(8,128)(2,1)}, bf16[528,128]{1,0:T(8,128)(2,1)S(1)}, u32[]{:S(2)}, u32[]{:S(2)}) %collective-permute-start.5) | collective-permute-done | bytes 135200 | tf_op jit(solution)/shard_map/ppermute | solution.py:900
  46.1 5.8 %collective-permute-start.11 = (bf16[528,128]{1,0:T(8,128)(2,1)}, bf16[528,128]{1,0:T(8,128)(2,1)S(1)}, u32[]{:S(2)}, u32[]{:S(2)}) collective-permute-start(bf16[528,128]{1,0:T(8,128)(2,1)} %get-tuple-element.98), channel_id=1, source_target_pairs={{0,12},{4,8},{8,4},{12,0},{16,28},{20,24},{24,20},{28,16},{1,13},{... | collective-permute-start | bytes 405512 | tf_op jit(solution)/shard_map/ppermute | solution.py:900
  52.0 3.9 %tree.2 = (bf16[528,128]{1,0:T(8,128)(2,1)}, bf16[528,128]{1,0:T(8,128)(2,1)}, bf16[528,128]{1,0:T(8,128)(2,1)}, bf16[528,128]{1,0:T(8,128)(2,1)}, bf16[528,128]...) custom-call(s32[2]{0:T(128)} %pad_add_fusion.place._, s32[8]{0:T(128)} %parents.3, ...), custom_call_target="tpu_custom_call" | custom-call | flops 10000000 | bytes 10000000 | tf_op jit(solution)/shard_map/tree/pallas_call | solution.py:631
  58.7 3.9 %tree.3 = (bf16[528,128]{1,0:T(8,128)(2,1)}, bf16[528,128]{1,0:T(8,128)(2,1)}, bf16[528,128]{1,0:T(8,128)(2,1)}, bf16[528,128]{1,0:T(8,128)(2,1)}, bf16[528,128]...) custom-call(s32[2]{0:T(128)} %pad_add_fusion.place._, s32[8]{0:T(128)} %parents.3, ...), custom_call_target="tpu_custom_call" | custom-call | flops 10000000 | bytes 10000000 | tf_op jit(solution)/shard_map/tree/pallas_call | solution.py:631
  65.3 3.8 %shard_map.122 = (bf16[256,256]{1,0:T(8,128)(2,1)}, bf16[256,256]{1,0:T(8,128)(2,1)}, f32[256,128]{1,0:T(8,128)}, f32[256,128]{1,0:T(8,128)}) custom-call(s32[2]{0:T(128)} %pad_add_fusion.place._, f32[1,4096]{1,0:T(1,128)} %broadcast_in_dim_reshape.3.__.refs_17_.refs_11_.refs_13_, bf16[256,1024]{1,0:T(8,128)(2,1)} %get-tuple-element.91.refs_0_.refs_6_, ...), custom_call_target="tpu_custom_call" | custom-call | flops 268435456 | bytes 2097152 | tf_op jit(solution)/shard_map/pallas_call | solution.py:558
  69.2 5.0 %shard_map.123 = (bf16[256,256]{1,0:T(8,128)(2,1)}, bf16[256,256]{1,0:T(8,128)(2,1)}, f32[256,128]{1,0:T(8,128)}, f32[256,128]{1,0:T(8,128)}) custom-call(s32[2]{0:T(128)} %pad_add_fusion.place._, f32[1,4096]{1,0:T(1,128)} %broadcast_in_dim_reshape.3.__.refs_17_.refs_11_.refs_13_, bf16[256,2048]{1,0:T(8,128)(2,1)} %get-tuple-element.117.refs_0_.refs_10_, ...), custom_call_target="tpu_custom_call" | custom-call | flops 536870912 | bytes 4194304 | tf_op jit(solution)/shard_map/pallas_call | solution.py:558
  74.3 3.1 %collective-permute-start.19 = (bf16[528,128]{1,0:T(8,128)(2,1)S(1)}, bf16[528,128]{1,0:T(8,128)(2,1)S(1)}, u32[]{:S(2)}, u32[]{:S(2)}) collective-permute-start(bf16[528,128]{1,0:T(8,128)(2,1)S(1)} %copy-done.37), channel_id=1, source_target_pairs={{0,20},{4,16},{8,28},{12,24},{16,4},{20,0},{24,12},{28,8},{1,21},{... | collective-permute-start | bytes 405512 | tf_op jit(solution)/shard_map/ppermute | solution.py:900
  79.9 2.2 %collective-permute-start.21 = (bf16[528,128]{1,0:T(8,128)(2,1)S(1)}, bf16[528,128]{1,0:T(8,128)(2,1)S(1)}, u32[]{:S(2)}, u32[]{:S(2)}) collective-permute-start(bf16[528,128]{1,0:T(8,128)(2,1)S(1)} %copy-done.40), channel_id=1, source_target_pairs={{0,28},{4,24},{8,20},{12,16},{16,12},{20,8},{24,4},{28,0},{1,29},{... | collective-permute-start | bytes 405512 | tf_op jit(solution)/shard_map/ppermute | solution.py:900
  82.1 9.3 %shard_map.124 = (bf16[256,4096]{1,0:T(8,128)(2,1)}, bf16[256,4096]{1,0:T(8,128)(2,1)}, f32[256,128]{1,0:T(8,128)}, bf16[2,64,128]{2,1,0:T(8,128)(2,1)}, bf16[2,...) custom-call(s32[2]{0:T(128)} %pad_add_fusion.place._, ...), custom_call_target="tpu_custom_call" | custom-call | flops 1610612736 | bytes 8388608 | tf_op jit(solution)/shard_map/pallas_call | solution.py:849
  91.4 19.1 %collective-permute-done.20.refs_0_ = bf16[528,128]{1,0:T(8,128)(2,1)S(1)} collective-permute-done((bf16[528,128]{1,0:T(8,128)(2,1)S(1)}, bf16[528,128]{1,0:T(8,128)(2,1)S(1)}, u32[]{:S(2)}, u32[]{:S(2)}) %collective-permute-start.20) | collective-permute-done | bytes 135200 | tf_op jit(solution)/shard_map/ppermute | solution.py:900
  114.6 4.7 %shard_map.125 = (bf16[256,4096]{1,0:T(8,128)(2,1)}, bf16[256,4096]{1,0:T(8,128)(2,1)}, f32[256,128]{1,0:T(8,128)}, f32[256,128]{1,0:T(8,128)}, f32[256,128]{1,0:T(8,128)}) custom-call(s32[2]{0:T(128)} %pad_add_fusion.place._, bf16[528,128]{1,0:T(8,128)(2,1)} %copy-done.16, ...), custom_call_target="tpu_custom_call", output_to_operand_aliasing={{0}: (14, {}), {1}: (15, {})} | custom-call | flops 805306368 | bytes 4194304 | tf_op jit(solution)/shard_map/pallas_call | solution.py:849
  120.1 6.3 %shard_map.126 = (bf16[256,4096]{1,0:T(8,128)(2,1)}, bf16[256,4096]{1,0:T(8,128)(2,1)}, f32[256,128]{1,0:T(8,128)}, f32[256,128]{1,0:T(8,128)}, f32[256,128]{1,0:T(8,128)}) custom-call(s32[2]{0:T(128)} %pad_add_fusion.place._, bf16[528,128]{1,0:T(8,128)(2,1)} %copy-done.23, ...), custom_call_target="tpu_custom_call", output_to_operand_aliasing={{0}: (16, {}), {1}: (17, {})} | custom-call | flops 805306368 | bytes 4194304 | tf_op jit(solution)/shard_map/pallas_call | solution.py:849
  127.1 3.1 %shard_map.128 = (bf16[2,64,128]{2,1,0:T(8,128)(2,1)}, bf16[2,64,128]{2,1,0:T(8,128)(2,1)}, bf16[2,64,128]{2,1,0:T(8,128)(2,1)}, bf16[2,64,128]{2,1,0:T(8,128)(2,1)}) custom-call(s32[2]{0:T(128)} %pad_add_fusion.place._, bf16[528,128]{1,0:T(8,128)(2,1)} %copy-done, bf16[528,128]{1,0:T(8,128)(2,1)} %copy-done.1, ...), custom_call_target="tpu_custom_call" | custom-call | flops 134217728 | bytes 2097152 | tf_op jit(solution)/shard_map/pallas_call | solution.py:711
  131.3 2.5 %collective-permute-start.33 = (bf16[2,64,128]{2,1,0:T(8,128)(2,1)}, bf16[2,64,128]{2,1,0:T(8,128)(2,1)S(1)}, u32[]{:S(2)}, u32[]{:S(2)}) collective-permute-start(bf16[2,64,128]{2,1,0:T(8,128)(2,1)} %get-tuple-element.148), channel_id=1, source_target_pairs={{0,3},{1,2},{2,1},{3,0},{4,7},{5,6},{6,5},{7,4},{8,11},{9,10},{10,... | collective-permute-start | bytes 98312 | tf_op jit(solution)/shard_map/ppermute | solution.py:900
  134.8 2.5 %collective-permute-start.30 = (bf16[2,64,128]{2,1,0:T(8,128)(2,1)S(1)}, bf16[2,64,128]{2,1,0:T(8,128)(2,1)S(1)}, u32[]{:S(2)}, u32[]{:S(2)}) collective-permute-start(bf16[2,64,128]{2,1,0:T(8,128)(2,1)S(1)} %copy-done.44), channel_id=1, source_target_pairs={{0,3},{1,2},{2,1},{3,0},{4,7},{5,6},{6,5},{7,4},{8,11},{9,10},{10,... | collective-permute-start | bytes 98312 | tf_op jit(solution)/shard_map/ppermute | solution.py:900
  137.3 4.7 %shard_map.127 = (bf16[256,4096]{1,0:T(8,128)(2,1)}, bf16[256,4096]{1,0:T(8,128)(2,1)}, f32[64,256]{1,0:T(8,128)}) custom-call(s32[2]{0:T(128)} %pad_add_fusion.place._, bf16[528,128]{1,0:T(8,128)(2,1)} %copy-done, bf16[528,128]{1,0:T(8,128)(2,1)} %copy-done.1, bf16[256,4096]{1,0:T(8,128)(2,1)} %bitcast.19, ...), custom_call_target="tpu_custom_call", output_to_operand_aliasing={{0}: (14, {}), {1}: (15, {})} | custom-call | flops 805306368 | bytes 4194304 | tf_op jit(solution)/shard_map/pallas_call | solution.py:849
  142.7 2.3 %place_grads.1 = (bf16[64,1024]{1,0:T(8,128)(2,1)}, bf16[64,1024]{1,0:T(8,128)(2,1)}) custom-call(s32[2]{0:T(128)} %pad_add_fusion.place._, bf16[2,64,128]{2,1,0:T(8,128)(2,1)} %get-tuple-element.139.refs_0_, bf16[2,64,128]{2,1,0:T(8,128)(2,1)} %copy-done.31, bf16[2,64,128]{2,1,0:T(8,128)(2,1)} %copy-done.32, bf16[2,64,128]{2,1,0:T(8,128)(2,1)} %copy-done.33, ...), custom_call_target="tpu_custom_call" | custom-call | tf_op jit(solution)/shard_map/place_grads/pallas_call | solution.py:885
  (154 shorter events, 26.5 us)
Async XLA Ops:
  6.1 20.3 %collective-permute-start.3 = (bf16[528,128]{1,0:T(8,128)(2,1)}, bf16[528,128]{1,0:T(8,128)(2,1)S(1)}, u32[]{:S(2)}, u32[]{:S(2)}) collective-permute-start(bf16[528,128]{1,0:T(8,128)(2,1)} %get-tuple-element.83), channel_id=1, source_target_pairs={{0,16},{4,20},{8,24},{12,28},{16,0},{20,4},{24,8},{28,12},{1,17},{... | collective-permute-start | bytes 405512 | tf_op jit(solution)/shard_map/ppermute | solution.py:900
  8.8 24.6 %collective-permute-start.4 = (bf16[528,128]{1,0:T(8,128)(2,1)}, bf16[528,128]{1,0:T(8,128)(2,1)S(1)}, u32[]{:S(2)}, u32[]{:S(2)}) collective-permute-start(bf16[528,128]{1,0:T(8,128)(2,1)} %get-tuple-element.84), channel_id=1, source_target_pairs={{0,20},{4,16},{8,28},{12,24},{16,4},{20,0},{24,12},{28,8},{1,21},{... | collective-permute-start | bytes 405512 | tf_op jit(solution)/shard_map/ppermute | solution.py:900
  8.8 26.2 %collective-permute-start.12 = (bf16[528,128]{1,0:T(8,128)(2,1)}, bf16[528,128]{1,0:T(8,128)(2,1)S(1)}, u32[]{:S(2)}, u32[]{:S(2)}) collective-permute-start(bf16[528,128]{1,0:T(8,128)(2,1)} %get-tuple-element.99), channel_id=1, source_target_pairs={{0,16},{4,20},{8,24},{12,28},{16,0},{20,4},{24,8},{28,12},{1,17},{... | collective-permute-start | bytes 405512 | tf_op jit(solution)/shard_map/ppermute | solution.py:900
  10.9 27.3 %collective-permute-start.13 = (bf16[528,128]{1,0:T(8,128)(2,1)}, bf16[528,128]{1,0:T(8,128)(2,1)S(1)}, u32[]{:S(2)}, u32[]{:S(2)}) collective-permute-start(bf16[528,128]{1,0:T(8,128)(2,1)} %get-tuple-element.100), channel_id=1, source_target_pairs={{0,20},{4,16},{8,28},{12,24},{16,4},{20,0},{24,12},{28,8},{1,21},{... | collective-permute-start | bytes 405512 | tf_op jit(solution)/shard_map/ppermute | solution.py:900
  16.1 25.6 %collective-permute-start.5 = (bf16[528,128]{1,0:T(8,128)(2,1)}, bf16[528,128]{1,0:T(8,128)(2,1)S(1)}, u32[]{:S(2)}, u32[]{:S(2)}) collective-permute-start(bf16[528,128]{1,0:T(8,128)(2,1)} %get-tuple-element.85), channel_id=1, source_target_pairs={{0,24},{4,28},{8,16},{12,20},{16,8},{20,12},{24,0},{28,4},{1,25},{... | collective-permute-start | bytes 405512 | tf_op jit(solution)/shard_map/ppermute | solution.py:900
  26.4 17.4 %collective-permute-start.6 = (bf16[528,128]{1,0:T(8,128)(2,1)}, bf16[528,128]{1,0:T(8,128)(2,1)S(1)}, u32[]{:S(2)}, u32[]{:S(2)}) collective-permute-start(bf16[528,128]{1,0:T(8,128)(2,1)} %get-tuple-element.86), channel_id=1, source_target_pairs={{0,28},{4,24},{8,20},{12,16},{16,12},{20,8},{24,4},{28,0},{1,29},{... | collective-permute-start | bytes 405512 | tf_op jit(solution)/shard_map/ppermute | solution.py:900
  33.4 12.4 %collective-permute-start = (bf16[528,128]{1,0:T(8,128)(2,1)}, bf16[528,128]{1,0:T(8,128)(2,1)S(1)}, u32[]{:S(2)}, u32[]{:S(2)}) collective-permute-start(bf16[528,128]{1,0:T(8,128)(2,1)} %get-tuple-element.80), channel_id=1, source_target_pairs={{0,4},{4,0},{8,12},{12,8},{16,20},{20,16},{24,28},{28,24},{1,5},{5... | collective-permute-start | bytes 405512 | tf_op jit(solution)/shard_map/ppermute | solution.py:900
  41.7 14.3 %collective-permute-start.14 = (bf16[528,128]{1,0:T(8,128)(2,1)S(1)}, bf16[528,128]{1,0:T(8,128)(2,1)S(1)}, u32[]{:S(2)}, u32[]{:S(2)}) collective-permute-start(bf16[528,128]{1,0:T(8,128)(2,1)S(1)} %copy-done.43), channel_id=1, source_target_pairs={{0,24},{4,28},{8,16},{12,20},{16,8},{20,12},{24,0},{28,4},{1,25},{... | collective-permute-start | bytes 405512 | tf_op jit(solution)/shard_map/ppermute | solution.py:900
  43.8 12.2 %collective-permute-start.15 = (bf16[528,128]{1,0:T(8,128)(2,1)S(1)}, bf16[528,128]{1,0:T(8,128)(2,1)S(1)}, u32[]{:S(2)}, u32[]{:S(2)}) collective-permute-start(bf16[528,128]{1,0:T(8,128)(2,1)S(1)} %copy-done.41), channel_id=1, source_target_pairs={{0,28},{4,24},{8,20},{12,16},{16,12},{20,8},{24,4},{28,0},{1,29},{... | collective-permute-start | bytes 405512 | tf_op jit(solution)/shard_map/ppermute | solution.py:900
  46.1 11.2 %collective-permute-start.10 = (bf16[528,128]{1,0:T(8,128)(2,1)}, bf16[528,128]{1,0:T(8,128)(2,1)S(1)}, u32[]{:S(2)}, u32[]{:S(2)}) collective-permute-start(bf16[528,128]{1,0:T(8,128)(2,1)} %get-tuple-element.97), channel_id=1, source_target_pairs={{0,8},{4,12},{8,0},{12,4},{16,24},{20,28},{24,16},{28,20},{1,9},{5... | collective-permute-start | bytes 405512 | tf_op jit(solution)/shard_map/ppermute | solution.py:900
  46.1 11.9 %collective-permute-start.11 = (bf16[528,128]{1,0:T(8,128)(2,1)}, bf16[528,128]{1,0:T(8,128)(2,1)S(1)}, u32[]{:S(2)}, u32[]{:S(2)}) collective-permute-start(bf16[528,128]{1,0:T(8,128)(2,1)} %get-tuple-element.98), channel_id=1, source_target_pairs={{0,12},{4,8},{8,4},{12,0},{16,28},{20,24},{24,20},{28,16},{1,13},{... | collective-permute-start | bytes 405512 | tf_op jit(solution)/shard_map/ppermute | solution.py:900
  56.2 18.1 %collective-permute-start.25 = (bf16[528,128]{1,0:T(8,128)(2,1)}, bf16[528,128]{1,0:T(8,128)(2,1)S(1)}, u32[]{:S(2)}, u32[]{:S(2)}) collective-permute-start(bf16[528,128]{1,0:T(8,128)(2,1)} %get-tuple-element.114), channel_id=1, source_target_pairs={{0,8},{4,12},{8,0},{12,4},{16,24},{20,28},{24,16},{28,20},{1,9},{5... | collective-permute-start | bytes 405512 | tf_op jit(solution)/shard_map/ppermute | solution.py:900
  57.3 20.2 %collective-permute-start.27 = (bf16[528,128]{1,0:T(8,128)(2,1)}, bf16[528,128]{1,0:T(8,128)(2,1)S(1)}, u32[]{:S(2)}, u32[]{:S(2)}) collective-permute-start(bf16[528,128]{1,0:T(8,128)(2,1)} %get-tuple-element.116), channel_id=1, source_target_pairs={{0,12},{4,8},{8,4},{12,0},{16,28},{20,24},{24,20},{28,16},{1,13},{... | collective-permute-start | bytes 405512 | tf_op jit(solution)/shard_map/ppermute | solution.py:900
  62.6 15.5 %collective-permute-start.22 = (bf16[528,128]{1,0:T(8,128)(2,1)}, bf16[528,128]{1,0:T(8,128)(2,1)S(1)}, u32[]{:S(2)}, u32[]{:S(2)}) collective-permute-start(bf16[528,128]{1,0:T(8,128)(2,1)} %get-tuple-element.111), channel_id=1, source_target_pairs={{0,4},{4,0},{8,12},{12,8},{16,20},{20,16},{24,28},{28,24},{1,5},{5... | collective-permute-start | bytes 405512 | tf_op jit(solution)/shard_map/ppermute | solution.py:900
  63.6 16.1 %collective-permute-start.24 = (bf16[528,128]{1,0:T(8,128)(2,1)}, bf16[528,128]{1,0:T(8,128)(2,1)S(1)}, u32[]{:S(2)}, u32[]{:S(2)}) collective-permute-start(bf16[528,128]{1,0:T(8,128)(2,1)} %get-tuple-element.113), channel_id=1, source_target_pairs={{0,8},{4,12},{8,0},{12,4},{16,24},{20,28},{24,16},{28,20},{1,9},{5... | collective-permute-start | bytes 405512 | tf_op jit(solution)/shard_map/ppermute | solution.py:900
  64.1 15.8 %collective-permute-start.26 = (bf16[528,128]{1,0:T(8,128)(2,1)}, bf16[528,128]{1,0:T(8,128)(2,1)S(1)}, u32[]{:S(2)}, u32[]{:S(2)}) collective-permute-start(bf16[528,128]{1,0:T(8,128)(2,1)} %get-tuple-element.115), channel_id=1, source_target_pairs={{0,12},{4,8},{8,4},{12,0},{16,28},{20,24},{24,20},{28,16},{1,13},{... | collective-permute-start | bytes 405512 | tf_op jit(solution)/shard_map/ppermute | solution.py:900
  74.3 45.0 %collective-permute-start.19 = (bf16[528,128]{1,0:T(8,128)(2,1)S(1)}, bf16[528,128]{1,0:T(8,128)(2,1)S(1)}, u32[]{:S(2)}, u32[]{:S(2)}) collective-permute-start(bf16[528,128]{1,0:T(8,128)(2,1)S(1)} %copy-done.37), channel_id=1, source_target_pairs={{0,20},{4,16},{8,28},{12,24},{16,4},{20,0},{24,12},{28,8},{1,21},{... | collective-permute-start | bytes 405512 | tf_op jit(solution)/shard_map/ppermute | solution.py:900
  77.4 41.9 %collective-permute-start.16 = (bf16[528,128]{1,0:T(8,128)(2,1)S(1)}, bf16[528,128]{1,0:T(8,128)(2,1)S(1)}, u32[]{:S(2)}, u32[]{:S(2)}) collective-permute-start(bf16[528,128]{1,0:T(8,128)(2,1)S(1)} %copy-done.39), channel_id=1, source_target_pairs={{0,16},{4,20},{8,24},{12,28},{16,0},{20,4},{24,8},{28,12},{1,17},{... | collective-permute-start | bytes 405512 | tf_op jit(solution)/shard_map/ppermute | solution.py:900
  78.1 41.2 %collective-permute-start.18 = (bf16[528,128]{1,0:T(8,128)(2,1)S(1)}, bf16[528,128]{1,0:T(8,128)(2,1)S(1)}, u32[]{:S(2)}, u32[]{:S(2)}) collective-permute-start(bf16[528,128]{1,0:T(8,128)(2,1)S(1)} %copy-done.38), channel_id=1, source_target_pairs={{0,20},{4,16},{8,28},{12,24},{16,4},{20,0},{24,12},{28,8},{1,21},{... | collective-permute-start | bytes 405512 | tf_op jit(solution)/shard_map/ppermute | solution.py:900
  79.7 30.8 %collective-permute-start.20 = (bf16[528,128]{1,0:T(8,128)(2,1)S(1)}, bf16[528,128]{1,0:T(8,128)(2,1)S(1)}, u32[]{:S(2)}, u32[]{:S(2)}) collective-permute-start(bf16[528,128]{1,0:T(8,128)(2,1)S(1)} %copy-done.42), channel_id=1, source_target_pairs={{0,24},{4,28},{8,16},{12,20},{16,8},{20,12},{24,0},{28,4},{1,25},{... | collective-permute-start | bytes 405512 | tf_op jit(solution)/shard_map/ppermute | solution.py:900
  79.9 32.8 %collective-permute-start.21 = (bf16[528,128]{1,0:T(8,128)(2,1)S(1)}, bf16[528,128]{1,0:T(8,128)(2,1)S(1)}, u32[]{:S(2)}, u32[]{:S(2)}) collective-permute-start(bf16[528,128]{1,0:T(8,128)(2,1)S(1)} %copy-done.40), channel_id=1, source_target_pairs={{0,28},{4,24},{8,20},{12,16},{16,12},{20,8},{24,4},{28,0},{1,29},{... | collective-permute-start | bytes 405512 | tf_op jit(solution)/shard_map/ppermute | solution.py:900
  110.5 15.9 %collective-permute-start.7 = (bf16[528,128]{1,0:T(8,128)(2,1)S(1)}, bf16[528,128]{1,0:T(8,128)(2,1)S(1)}, u32[]{:S(2)}, u32[]{:S(2)}) collective-permute-start(bf16[528,128]{1,0:T(8,128)(2,1)S(1)} %copy-done.36), channel_id=1, source_target_pairs={{0,24},{4,28},{8,16},{12,20},{16,8},{20,12},{24,0},{28,4},{1,25},{... | collective-permute-start | bytes 405512 | tf_op jit(solution)/shard_map/ppermute | solution.py:900
  112.7 13.7 %collective-permute-start.8 = (bf16[528,128]{1,0:T(8,128)(2,1)S(1)}, bf16[528,128]{1,0:T(8,128)(2,1)S(1)}, u32[]{:S(2)}, u32[]{:S(2)}) collective-permute-start(bf16[528,128]{1,0:T(8,128)(2,1)S(1)} %copy-done.35), channel_id=1, source_target_pairs={{0,28},{4,24},{8,20},{12,16},{16,12},{20,8},{24,4},{28,0},{1,29},{... | collective-permute-start | bytes 405512 | tf_op jit(solution)/shard_map/ppermute | solution.py:900
  130.8 11.2 %collective-permute-start.32 = (bf16[2,64,128]{2,1,0:T(8,128)(2,1)}, bf16[2,64,128]{2,1,0:T(8,128)(2,1)S(1)}, u32[]{:S(2)}, u32[]{:S(2)}) collective-permute-start(bf16[2,64,128]{2,1,0:T(8,128)(2,1)} %get-tuple-element.147), channel_id=1, source_target_pairs={{0,2},{1,3},{2,0},{3,1},{4,6},{5,7},{6,4},{7,5},{8,10},{9,11},{10,... | collective-permute-start | bytes 98312 | tf_op jit(solution)/shard_map/ppermute | solution.py:900
  (57 other events, 447.6 us)
